TPU v7x, 256 devices: a whole 4x4x8 slice. The times are simulated.
256 devices in a mesh: rows: 64 (over z, x, y_lo), grp: 4 (over y_hi, core).
Axes of the slice: x: 4, y: 4 (y_hi: 2, y_lo: 2; y = y_hi * 2 + y_lo), z: 8, core: 2. Of those that a mesh axis runs over, the one named last changes fastest.
Arguments:
- visibilities: float32 [2, 1048576], P(None, ('rows', 'grp')), may hold values from -6 to 6
- uv_tiles: int32 [2, 1048576], P(None, ('rows', 'grp')), may hold values from 0 to 511, as said below
- kernel_offsets: int32 [2, 1048576], P(None, ('rows', 'grp')), may hold values from 0 to 7
- kernel: float32 [8, 8], replicated, may hold values from 0.5 to 1.5
Outputs:
- dirty_image: float32 [2, 4096, 4096], P(None, ('rows', 'grp'))
Inputs may be any that keep to these rules, and one draw needn't show every extreme that they name: `uv_tiles`: row 0 holds tile rows, row 1 tile columns. The visibilities of baseline block q (positions q * 4096 to (q + 1) * 4096 - 1), with s = q divided by the number of devices of grp, have tile rows from s * 8 to (s + 1) * 8 - 1.
All inputs are finite; a program needn't handle non-finite values.
Results may differ from a plain program's by a relative error of at most 0.0044.
Values sent between devices are 32-bit elements; how exact they have to be, the bound alone decides.
A program may use at most 64 MiB of HBM per device.

v0:
```python
import math

import jax
import jax.numpy as jnp
from jax import lax
from jax.sharding import PartitionSpec as P

G = 4096


vis_block = 256


def passed_along(x, axis, by):
    peers = lax.axis_size(axis)
    return lax.ppermute(x, axis, [(i, (i + by) % peers) for i in range(peers)])


def cut_along(x, dim, peers):
    before, after = (x.shape[:dim], x.shape[dim + 1 :])
    return jnp.moveaxis(x.reshape(*before, peers, -1, *after), dim, 0)


def sent_and_summed(x, axis, dim):
    tiles = cut_along(x, dim, lax.axis_size(axis))
    arrived = lax.all_to_all(tiles, axis, split_axis=0, concat_axis=0, tiled=True)
    return arrived.sum(axis=0)


def laid_out(tiles, dim):
    tiles = jnp.moveaxis(tiles, 0, dim)
    shape = tiles.shape
    return tiles.reshape(*shape[:dim], shape[dim] * shape[dim + 1], *shape[dim + 2 :])


def one_exchange(x, axis, axes, splits, concats):
    sizes = [lax.axis_size(a) for a in axes]
    tiles = cut_along(x, splits[0], sizes[0])
    tiles = jnp.moveaxis(cut_along(tiles, splits[1] + 1, sizes[1]), 0, 1)
    inside = tiles.shape[2:]
    tiles = tiles.reshape(-1, *inside)
    tiles = lax.all_to_all(tiles, axis, split_axis=0, concat_axis=0, tiled=True)
    tiles = laid_out(tiles.reshape(*sizes, *inside), concats[0] + 1)
    return laid_out(tiles, concats[1])


def phase_table(first_count, second_count, length):
    first_ids = lax.broadcasted_iota(jnp.int32, (first_count, second_count), 0)
    second_ids = lax.broadcasted_iota(jnp.int32, (first_count, second_count), 1)
    angles = (first_ids * second_ids % length).astype(jnp.float32) * (2.0 * math.pi / length)
    return (jnp.cos(angles), jnp.sin(angles))


def complex_einsum(pattern, left_pair, right_pair):

    def product(left_one, right_one):
        return jnp.einsum(pattern, left_one, right_one, precision=lax.Precision.HIGHEST)

    real_out = product(left_pair[0], right_pair[0]) - product(left_pair[1], right_pair[1])
    imag_out = product(left_pair[0], right_pair[1]) + product(left_pair[1], right_pair[0])
    return (real_out, imag_out)


def complex_scale(operand, factor):
    return (
        operand[0] * factor[0] - operand[1] * factor[1],
        operand[0] * factor[1] + operand[1] * factor[0],
    )


def grid_window(visibilities, uv_tiles, kernel_offsets, kernel, row_list, grid_side, block_size):
    vis_count = visibilities.shape[1]
    tap_count = kernel.shape[0]
    window_rows = row_list.shape[0]
    tap_ids = lax.broadcasted_iota(jnp.int32, (1, tap_count), 1)
    row_ids = jnp.broadcast_to(row_list[None, :], (block_size, window_rows))
    col_ids = lax.broadcasted_iota(jnp.int32, (block_size, grid_side), 1)

    def lookup(offsets):
        one_hot = (offsets[:, None] == tap_ids).astype(jnp.float32)
        return jnp.dot(one_hot, kernel, precision=lax.Precision.HIGHEST)

    def add_block(block_index, accumulated):
        block_start = block_index * block_size

        def take_block(values):
            return lax.dynamic_slice_in_dim(values, block_start, block_size, 1)

        vis_now = take_block(visibilities)
        tiles_now = take_block(uv_tiles)
        offsets_now = take_block(kernel_offsets)
        row_start = tap_count * tiles_now[0] + offsets_now[0]
        col_start = tap_count * tiles_now[1] + offsets_now[1]
        kern_rows = lookup(offsets_now[0])
        kern_cols = lookup(offsets_now[1])
        row_delta = row_ids - row_start[:, None]
        col_delta = (col_ids - col_start[:, None]) % grid_side
        row_weight = jnp.zeros(row_ids.shape, jnp.float32)
        col_weight = jnp.zeros(col_ids.shape, jnp.float32)
        for tap_index in range(tap_count):
            row_weight = jnp.where(
                row_delta == tap_index, kern_rows[:, tap_index : tap_index + 1], row_weight
            )
            col_weight = jnp.where(
                col_delta == tap_index, kern_cols[:, tap_index : tap_index + 1], col_weight
            )
        row_weight = row_weight.astype(jnp.bfloat16)
        col_values = jnp.concatenate(
            [
                (vis_now[0][:, None] * col_weight).astype(jnp.bfloat16),
                (vis_now[1][:, None] * col_weight).astype(jnp.bfloat16),
            ],
            axis=1,
        )
        return accumulated + lax.dot_general(
            row_weight, col_values, (((0,), (0,)), ((), ())), preferred_element_type=jnp.float32
        )

    initial = jnp.zeros((window_rows, 2 * grid_side), jnp.float32)
    return lax.fori_loop(0, vis_count // block_size, add_block, initial)


def row_spectra(row_slab, rows_count, height, grid_side):
    line_count = row_slab.shape[0]
    real_part = row_slab[:, :grid_side].reshape(line_count, height, rows_count)
    imag_part = row_slab[:, grid_side:].reshape(line_count, height, rows_count)
    section_one = complex_einsum(
        "jrm,rk->jkm", (real_part, imag_part), phase_table(height, height, height)
    )
    turned = complex_scale(section_one, phase_table(height, rows_count, grid_side))
    return complex_einsum("jkm,mq->qkj", turned, phase_table(rows_count, rows_count, rows_count))


def column_spectra(columns, layout, rows_count, group_count, height, grid_side):
    columns_dev = height // group_count
    turned_layout = layout.replace("r", "k")
    section_one = complex_einsum(
        layout + ",rk->" + turned_layout, columns, phase_table(rows_count, rows_count, rows_count)
    )
    twiddles = tuple(
        (
            t.reshape(rows_count, group_count, columns_dev)
            for t in phase_table(rows_count, height, grid_side)
        )
    )
    twiddles = tuple((t[:, :, None] for t in twiddles))
    turned = complex_scale(section_one, twiddles)
    section_table = tuple(
        (t.reshape(group_count, columns_dev, height) for t in phase_table(height, height, height))
    )
    result = complex_einsum(turned_layout + ",gjq->cqk", turned, section_table)
    inverse_side = 1.0 / grid_side
    return jnp.stack(
        [part_out.reshape(columns_dev, grid_side) * inverse_side for part_out in result]
    )


def shards(visibilities, uv_tiles, kernel_offsets, kernel):
    rows_count = lax.axis_size("rows")
    group_count = lax.axis_size("grp")
    grid_side = G
    height = grid_side // rows_count
    columns_dev = height // group_count
    tap_count = kernel.shape[0]
    block_size = min(vis_block, visibilities.shape[1])
    row_base = lax.axis_index("rows") * height
    row_list = row_base + jnp.arange(height + tap_count, dtype=jnp.int32)
    partial_grid = grid_window(
        visibilities, uv_tiles, kernel_offsets, kernel, row_list, grid_side, block_size
    )
    main_rows = partial_grid[:height]
    tail_rows = partial_grid[height:]
    spill_rows = passed_along(tail_rows, "rows", 1)
    row_slab = jnp.concatenate([main_rows[:tap_count] + spill_rows, main_rows[tap_count:]], axis=0)
    own_rows = sent_and_summed(row_slab, "grp", 0)
    spectra = row_spectra(own_rows, rows_count, height, grid_side)
    send_blocks = tuple(
        (p.reshape(rows_count, group_count, columns_dev * columns_dev) for p in spectra)
    )
    received = jax.tree.map(
        lambda part: one_exchange(part, ("rows", "grp"), ("rows", "grp"), (0, 1), (0, 1)),
        send_blocks,
    )
    columns = tuple(
        (p.reshape(rows_count, group_count, columns_dev, columns_dev) for p in received)
    )
    layout = "rgcj"
    return column_spectra(columns, layout, rows_count, group_count, height, grid_side)


def solution(mesh):
    in_specs = (P(None, ("rows", "grp")), P(None, ("rows", "grp")), P(None, ("rows", "grp")), P())
    out_specs = P(None, ("rows", "grp"), None)
    return jax.shard_map(shards, mesh=mesh, in_specs=in_specs, out_specs=out_specs, check_vma=False)
```

profile of v0, /device:TPU:1, one launch (start us, length us, event | category | flops | bytes accessed | tf_op | source)
XLA Modules:
  0.0 347.2 jit_solution(15845289249195009163)
XLA Ops:
  0.0 235.0 %while.17 = (s32[]{:T(128)}, f32[72,8192]{1,0:T(8,128)}, s32[2,4096]{1,0:T(2,128)}, s32[2,4096]{1,0:T(2,128)}, f32[8,8]{1,0:T(8,128)}, /*index=5*/f32[2,4096]{1,...) while((s32[]{:T(128)}, f32[72,8192]{1,0:T(8,128)}, ...), condition=%wide.region_1.2_spmd.clone.clone, body=%wide.region_0.1_spmd.clone.clone.sunk | while | flops 345824256 | bytes 13199365 | solution.py:120
  2.7 6.8 %multiply_convert_fusion.3 = (bf16[256,4096]{1,0:T(8,128)(2,1)S(1)}, bf16[256,4096]{1,0:T(8,128)(2,1)}) fusion(f32[256]{0:T(256)S(1)} %bitcast.217, f32[256]{0:T(256)S(1)} %bitcast.218, f32[256]{0:T(256)S(1)} %bitcast.219, f32[256]{0:T(256)S(1)} %bitcast.220, f32[256]{0:T(256)S(1)} %bitcast.221, f32[256]{0:T(256)S(1)} %bitcast.222, ...), kind=kLoop, calls=%fused_computation.15.clone.1 | loop fusion | flops 33554432 | bytes 4205568 | tf_op jit(solution)/shard_map/while/body/eval_jaxpr/convert_element_type | solution.py:110
  9.8 4.3 %convolution_add_fusion.4 = f32[72,8192]{1,0:T(8,128)} fusion(bf16[256,4096]{1,0:T(8,128)(2,1)} %get-tuple-element.410, bf16[256,4096]{1,0:T(8,128)(2,1)S(1)} %get-tuple-element.411, f32[72,8192]{1,0:T(8,128)} %get-tuple-element.435, pred[]{:T(512)S(6)} %compare.18, s32[72]{0:T(128)S(1)} %get-tuple-element.452, f32[256]{0:T(256)S(1)} %bitcast.227, ...), kind=kOutput, calls=%fused_computation.3.clone.1 | convolution fusion | flops 311871488 | bytes 8922401 | tf_op jit(solution)/shard_map/while/body/eval_jaxpr/dot_general | solution.py:115
  16.7 6.8 %multiply_convert_fusion.3 = (bf16[256,4096]{1,0:T(8,128)(2,1)S(1)}, bf16[256,4096]{1,0:T(8,128)(2,1)}) fusion(f32[256]{0:T(256)S(1)} %bitcast.217, f32[256]{0:T(256)S(1)} %bitcast.218, f32[256]{0:T(256)S(1)} %bitcast.219, f32[256]{0:T(256)S(1)} %bitcast.220, f32[256]{0:T(256)S(1)} %bitcast.221, f32[256]{0:T(256)S(1)} %bitcast.222, ...), kind=kLoop, calls=%fused_computation.15.clone.1 | loop fusion | flops 33554432 | bytes 4205568 | tf_op jit(solution)/shard_map/while/body/eval_jaxpr/convert_element_type | solution.py:110
  23.8 5.0 %convolution_add_fusion.4 = f32[72,8192]{1,0:T(8,128)} fusion(bf16[256,4096]{1,0:T(8,128)(2,1)} %get-tuple-element.410, bf16[256,4096]{1,0:T(8,128)(2,1)S(1)} %get-tuple-element.411, f32[72,8192]{1,0:T(8,128)} %get-tuple-element.435, pred[]{:T(512)S(6)} %compare.18, s32[72]{0:T(128)S(1)} %get-tuple-element.452, f32[256]{0:T(256)S(1)} %bitcast.227, ...), kind=kOutput, calls=%fused_computation.3.clone.1 | convolution fusion | flops 311871488 | bytes 8922401 | tf_op jit(solution)/shard_map/while/body/eval_jaxpr/dot_general | solution.py:115
  31.4 6.8 %multiply_convert_fusion.3 = (bf16[256,4096]{1,0:T(8,128)(2,1)S(1)}, bf16[256,4096]{1,0:T(8,128)(2,1)}) fusion(f32[256]{0:T(256)S(1)} %bitcast.217, f32[256]{0:T(256)S(1)} %bitcast.218, f32[256]{0:T(256)S(1)} %bitcast.219, f32[256]{0:T(256)S(1)} %bitcast.220, f32[256]{0:T(256)S(1)} %bitcast.221, f32[256]{0:T(256)S(1)} %bitcast.222, ...), kind=kLoop, calls=%fused_computation.15.clone.1 | loop fusion | flops 33554432 | bytes 4205568 | tf_op jit(solution)/shard_map/while/body/eval_jaxpr/convert_element_type | solution.py:110
  38.5 5.0 %convolution_add_fusion.4 = f32[72,8192]{1,0:T(8,128)} fusion(bf16[256,4096]{1,0:T(8,128)(2,1)} %get-tuple-element.410, bf16[256,4096]{1,0:T(8,128)(2,1)S(1)} %get-tuple-element.411, f32[72,8192]{1,0:T(8,128)} %get-tuple-element.435, pred[]{:T(512)S(6)} %compare.18, s32[72]{0:T(128)S(1)} %get-tuple-element.452, f32[256]{0:T(256)S(1)} %bitcast.227, ...), kind=kOutput, calls=%fused_computation.3.clone.1 | convolution fusion | flops 311871488 | bytes 8922401 | tf_op jit(solution)/shard_map/while/body/eval_jaxpr/dot_general | solution.py:115
  46.2 6.8 %multiply_convert_fusion.3 = (bf16[256,4096]{1,0:T(8,128)(2,1)S(1)}, bf16[256,4096]{1,0:T(8,128)(2,1)}) fusion(f32[256]{0:T(256)S(1)} %bitcast.217, f32[256]{0:T(256)S(1)} %bitcast.218, f32[256]{0:T(256)S(1)} %bitcast.219, f32[256]{0:T(256)S(1)} %bitcast.220, f32[256]{0:T(256)S(1)} %bitcast.221, f32[256]{0:T(256)S(1)} %bitcast.222, ...), kind=kLoop, calls=%fused_computation.15.clone.1 | loop fusion | flops 33554432 | bytes 4205568 | tf_op jit(solution)/shard_map/while/body/eval_jaxpr/convert_element_type | solution.py:110
  53.3 5.0 %convolution_add_fusion.4 = f32[72,8192]{1,0:T(8,128)} fusion(bf16[256,4096]{1,0:T(8,128)(2,1)} %get-tuple-element.410, bf16[256,4096]{1,0:T(8,128)(2,1)S(1)} %get-tuple-element.411, f32[72,8192]{1,0:T(8,128)} %get-tuple-element.435, pred[]{:T(512)S(6)} %compare.18, s32[72]{0:T(128)S(1)} %get-tuple-element.452, f32[256]{0:T(256)S(1)} %bitcast.227, ...), kind=kOutput, calls=%fused_computation.3.clone.1 | convolution fusion | flops 311871488 | bytes 8922401 | tf_op jit(solution)/shard_map/while/body/eval_jaxpr/dot_general | solution.py:115
  60.9 6.8 %multiply_convert_fusion.3 = (bf16[256,4096]{1,0:T(8,128)(2,1)S(1)}, bf16[256,4096]{1,0:T(8,128)(2,1)}) fusion(f32[256]{0:T(256)S(1)} %bitcast.217, f32[256]{0:T(256)S(1)} %bitcast.218, f32[256]{0:T(256)S(1)} %bitcast.219, f32[256]{0:T(256)S(1)} %bitcast.220, f32[256]{0:T(256)S(1)} %bitcast.221, f32[256]{0:T(256)S(1)} %bitcast.222, ...), kind=kLoop, calls=%fused_computation.15.clone.1 | loop fusion | flops 33554432 | bytes 4205568 | tf_op jit(solution)/shard_map/while/body/eval_jaxpr/convert_element_type | solution.py:110
  68.0 5.0 %convolution_add_fusion.4 = f32[72,8192]{1,0:T(8,128)} fusion(bf16[256,4096]{1,0:T(8,128)(2,1)} %get-tuple-element.410, bf16[256,4096]{1,0:T(8,128)(2,1)S(1)} %get-tuple-element.411, f32[72,8192]{1,0:T(8,128)} %get-tuple-element.435, pred[]{:T(512)S(6)} %compare.18, s32[72]{0:T(128)S(1)} %get-tuple-element.452, f32[256]{0:T(256)S(1)} %bitcast.227, ...), kind=kOutput, calls=%fused_computation.3.clone.1 | convolution fusion | flops 311871488 | bytes 8922401 | tf_op jit(solution)/shard_map/while/body/eval_jaxpr/dot_general | solution.py:115
  75.6 6.8 %multiply_convert_fusion.3 = (bf16[256,4096]{1,0:T(8,128)(2,1)S(1)}, bf16[256,4096]{1,0:T(8,128)(2,1)}) fusion(f32[256]{0:T(256)S(1)} %bitcast.217, f32[256]{0:T(256)S(1)} %bitcast.218, f32[256]{0:T(256)S(1)} %bitcast.219, f32[256]{0:T(256)S(1)} %bitcast.220, f32[256]{0:T(256)S(1)} %bitcast.221, f32[256]{0:T(256)S(1)} %bitcast.222, ...), kind=kLoop, calls=%fused_computation.15.clone.1 | loop fusion | flops 33554432 | bytes 4205568 | tf_op jit(solution)/shard_map/while/body/eval_jaxpr/convert_element_type | solution.py:110
  82.7 5.0 %convolution_add_fusion.4 = f32[72,8192]{1,0:T(8,128)} fusion(bf16[256,4096]{1,0:T(8,128)(2,1)} %get-tuple-element.410, bf16[256,4096]{1,0:T(8,128)(2,1)S(1)} %get-tuple-element.411, f32[72,8192]{1,0:T(8,128)} %get-tuple-element.435, pred[]{:T(512)S(6)} %compare.18, s32[72]{0:T(128)S(1)} %get-tuple-element.452, f32[256]{0:T(256)S(1)} %bitcast.227, ...), kind=kOutput, calls=%fused_computation.3.clone.1 | convolution fusion | flops 311871488 | bytes 8922401 | tf_op jit(solution)/shard_map/while/body/eval_jaxpr/dot_general | solution.py:115
  90.4 6.8 %multiply_convert_fusion.3 = (bf16[256,4096]{1,0:T(8,128)(2,1)S(1)}, bf16[256,4096]{1,0:T(8,128)(2,1)}) fusion(f32[256]{0:T(256)S(1)} %bitcast.217, f32[256]{0:T(256)S(1)} %bitcast.218, f32[256]{0:T(256)S(1)} %bitcast.219, f32[256]{0:T(256)S(1)} %bitcast.220, f32[256]{0:T(256)S(1)} %bitcast.221, f32[256]{0:T(256)S(1)} %bitcast.222, ...), kind=kLoop, calls=%fused_computation.15.clone.1 | loop fusion | flops 33554432 | bytes 4205568 | tf_op jit(solution)/shard_map/while/body/eval_jaxpr/convert_element_type | solution.py:110
  97.5 5.0 %convolution_add_fusion.4 = f32[72,8192]{1,0:T(8,128)} fusion(bf16[256,4096]{1,0:T(8,128)(2,1)} %get-tuple-element.410, bf16[256,4096]{1,0:T(8,128)(2,1)S(1)} %get-tuple-element.411, f32[72,8192]{1,0:T(8,128)} %get-tuple-element.435, pred[]{:T(512)S(6)} %compare.18, s32[72]{0:T(128)S(1)} %get-tuple-element.452, f32[256]{0:T(256)S(1)} %bitcast.227, ...), kind=kOutput, calls=%fused_computation.3.clone.1 | convolution fusion | flops 311871488 | bytes 8922401 | tf_op jit(solution)/shard_map/while/body/eval_jaxpr/dot_general | solution.py:115
  105.1 6.8 %multiply_convert_fusion.3 = (bf16[256,4096]{1,0:T(8,128)(2,1)S(1)}, bf16[256,4096]{1,0:T(8,128)(2,1)}) fusion(f32[256]{0:T(256)S(1)} %bitcast.217, f32[256]{0:T(256)S(1)} %bitcast.218, f32[256]{0:T(256)S(1)} %bitcast.219, f32[256]{0:T(256)S(1)} %bitcast.220, f32[256]{0:T(256)S(1)} %bitcast.221, f32[256]{0:T(256)S(1)} %bitcast.222, ...), kind=kLoop, calls=%fused_computation.15.clone.1 | loop fusion | flops 33554432 | bytes 4205568 | tf_op jit(solution)/shard_map/while/body/eval_jaxpr/convert_element_type | solution.py:110
  112.2 5.0 %convolution_add_fusion.4 = f32[72,8192]{1,0:T(8,128)} fusion(bf16[256,4096]{1,0:T(8,128)(2,1)} %get-tuple-element.410, bf16[256,4096]{1,0:T(8,128)(2,1)S(1)} %get-tuple-element.411, f32[72,8192]{1,0:T(8,128)} %get-tuple-element.435, pred[]{:T(512)S(6)} %compare.18, s32[72]{0:T(128)S(1)} %get-tuple-element.452, f32[256]{0:T(256)S(1)} %bitcast.227, ...), kind=kOutput, calls=%fused_computation.3.clone.1 | convolution fusion | flops 311871488 | bytes 8922401 | tf_op jit(solution)/shard_map/while/body/eval_jaxpr/dot_general | solution.py:115
  119.8 6.8 %multiply_convert_fusion.3 = (bf16[256,4096]{1,0:T(8,128)(2,1)S(1)}, bf16[256,4096]{1,0:T(8,128)(2,1)}) fusion(f32[256]{0:T(256)S(1)} %bitcast.217, f32[256]{0:T(256)S(1)} %bitcast.218, f32[256]{0:T(256)S(1)} %bitcast.219, f32[256]{0:T(256)S(1)} %bitcast.220, f32[256]{0:T(256)S(1)} %bitcast.221, f32[256]{0:T(256)S(1)} %bitcast.222, ...), kind=kLoop, calls=%fused_computation.15.clone.1 | loop fusion | flops 33554432 | bytes 4205568 | tf_op jit(solution)/shard_map/while/body/eval_jaxpr/convert_element_type | solution.py:110
  126.9 5.0 %convolution_add_fusion.4 = f32[72,8192]{1,0:T(8,128)} fusion(bf16[256,4096]{1,0:T(8,128)(2,1)} %get-tuple-element.410, bf16[256,4096]{1,0:T(8,128)(2,1)S(1)} %get-tuple-element.411, f32[72,8192]{1,0:T(8,128)} %get-tuple-element.435, pred[]{:T(512)S(6)} %compare.18, s32[72]{0:T(128)S(1)} %get-tuple-element.452, f32[256]{0:T(256)S(1)} %bitcast.227, ...), kind=kOutput, calls=%fused_computation.3.clone.1 | convolution fusion | flops 311871488 | bytes 8922401 | tf_op jit(solution)/shard_map/while/body/eval_jaxpr/dot_general | solution.py:115
  134.6 6.8 %multiply_convert_fusion.3 = (bf16[256,4096]{1,0:T(8,128)(2,1)S(1)}, bf16[256,4096]{1,0:T(8,128)(2,1)}) fusion(f32[256]{0:T(256)S(1)} %bitcast.217, f32[256]{0:T(256)S(1)} %bitcast.218, f32[256]{0:T(256)S(1)} %bitcast.219, f32[256]{0:T(256)S(1)} %bitcast.220, f32[256]{0:T(256)S(1)} %bitcast.221, f32[256]{0:T(256)S(1)} %bitcast.222, ...), kind=kLoop, calls=%fused_computation.15.clone.1 | loop fusion | flops 33554432 | bytes 4205568 | tf_op jit(solution)/shard_map/while/body/eval_jaxpr/convert_element_type | solution.py:110
  141.7 5.0 %convolution_add_fusion.4 = f32[72,8192]{1,0:T(8,128)} fusion(bf16[256,4096]{1,0:T(8,128)(2,1)} %get-tuple-element.410, bf16[256,4096]{1,0:T(8,128)(2,1)S(1)} %get-tuple-element.411, f32[72,8192]{1,0:T(8,128)} %get-tuple-element.435, pred[]{:T(512)S(6)} %compare.18, s32[72]{0:T(128)S(1)} %get-tuple-element.452, f32[256]{0:T(256)S(1)} %bitcast.227, ...), kind=kOutput, calls=%fused_computation.3.clone.1 | convolution fusion | flops 311871488 | bytes 8922401 | tf_op jit(solution)/shard_map/while/body/eval_jaxpr/dot_general | solution.py:115
  149.3 6.8 %multiply_convert_fusion.3 = (bf16[256,4096]{1,0:T(8,128)(2,1)S(1)}, bf16[256,4096]{1,0:T(8,128)(2,1)}) fusion(f32[256]{0:T(256)S(1)} %bitcast.217, f32[256]{0:T(256)S(1)} %bitcast.218, f32[256]{0:T(256)S(1)} %bitcast.219, f32[256]{0:T(256)S(1)} %bitcast.220, f32[256]{0:T(256)S(1)} %bitcast.221, f32[256]{0:T(256)S(1)} %bitcast.222, ...), kind=kLoop, calls=%fused_computation.15.clone.1 | loop fusion | flops 33554432 | bytes 4205568 | tf_op jit(solution)/shard_map/while/body/eval_jaxpr/convert_element_type | solution.py:110
  156.4 5.0 %convolution_add_fusion.4 = f32[72,8192]{1,0:T(8,128)} fusion(bf16[256,4096]{1,0:T(8,128)(2,1)} %get-tuple-element.410, bf16[256,4096]{1,0:T(8,128)(2,1)S(1)} %get-tuple-element.411, f32[72,8192]{1,0:T(8,128)} %get-tuple-element.435, pred[]{:T(512)S(6)} %compare.18, s32[72]{0:T(128)S(1)} %get-tuple-element.452, f32[256]{0:T(256)S(1)} %bitcast.227, ...), kind=kOutput, calls=%fused_computation.3.clone.1 | convolution fusion | flops 311871488 | bytes 8922401 | tf_op jit(solution)/shard_map/while/body/eval_jaxpr/dot_general | solution.py:115
  164.0 6.8 %multiply_convert_fusion.3 = (bf16[256,4096]{1,0:T(8,128)(2,1)S(1)}, bf16[256,4096]{1,0:T(8,128)(2,1)}) fusion(f32[256]{0:T(256)S(1)} %bitcast.217, f32[256]{0:T(256)S(1)} %bitcast.218, f32[256]{0:T(256)S(1)} %bitcast.219, f32[256]{0:T(256)S(1)} %bitcast.220, f32[256]{0:T(256)S(1)} %bitcast.221, f32[256]{0:T(256)S(1)} %bitcast.222, ...), kind=kLoop, calls=%fused_computation.15.clone.1 | loop fusion | flops 33554432 | bytes 4205568 | tf_op jit(solution)/shard_map/while/body/eval_jaxpr/convert_element_type | solution.py:110
  171.1 5.0 %convolution_add_fusion.4 = f32[72,8192]{1,0:T(8,128)} fusion(bf16[256,4096]{1,0:T(8,128)(2,1)} %get-tuple-element.410, bf16[256,4096]{1,0:T(8,128)(2,1)S(1)} %get-tuple-element.411, f32[72,8192]{1,0:T(8,128)} %get-tuple-element.435, pred[]{:T(512)S(6)} %compare.18, s32[72]{0:T(128)S(1)} %get-tuple-element.452, f32[256]{0:T(256)S(1)} %bitcast.227, ...), kind=kOutput, calls=%fused_computation.3.clone.1 | convolution fusion | flops 311871488 | bytes 8922401 | tf_op jit(solution)/shard_map/while/body/eval_jaxpr/dot_general | solution.py:115
  178.8 6.8 %multiply_convert_fusion.3 = (bf16[256,4096]{1,0:T(8,128)(2,1)S(1)}, bf16[256,4096]{1,0:T(8,128)(2,1)}) fusion(f32[256]{0:T(256)S(1)} %bitcast.217, f32[256]{0:T(256)S(1)} %bitcast.218, f32[256]{0:T(256)S(1)} %bitcast.219, f32[256]{0:T(256)S(1)} %bitcast.220, f32[256]{0:T(256)S(1)} %bitcast.221, f32[256]{0:T(256)S(1)} %bitcast.222, ...), kind=kLoop, calls=%fused_computation.15.clone.1 | loop fusion | flops 33554432 | bytes 4205568 | tf_op jit(solution)/shard_map/while/body/eval_jaxpr/convert_element_type | solution.py:110
  185.9 5.0 %convolution_add_fusion.4 = f32[72,8192]{1,0:T(8,128)} fusion(bf16[256,4096]{1,0:T(8,128)(2,1)} %get-tuple-element.410, bf16[256,4096]{1,0:T(8,128)(2,1)S(1)} %get-tuple-element.411, f32[72,8192]{1,0:T(8,128)} %get-tuple-element.435, pred[]{:T(512)S(6)} %compare.18, s32[72]{0:T(128)S(1)} %get-tuple-element.452, f32[256]{0:T(256)S(1)} %bitcast.227, ...), kind=kOutput, calls=%fused_computation.3.clone.1 | convolution fusion | flops 311871488 | bytes 8922401 | tf_op jit(solution)/shard_map/while/body/eval_jaxpr/dot_general | solution.py:115
  193.5 6.8 %multiply_convert_fusion.3 = (bf16[256,4096]{1,0:T(8,128)(2,1)S(1)}, bf16[256,4096]{1,0:T(8,128)(2,1)}) fusion(f32[256]{0:T(256)S(1)} %bitcast.217, f32[256]{0:T(256)S(1)} %bitcast.218, f32[256]{0:T(256)S(1)} %bitcast.219, f32[256]{0:T(256)S(1)} %bitcast.220, f32[256]{0:T(256)S(1)} %bitcast.221, f32[256]{0:T(256)S(1)} %bitcast.222, ...), kind=kLoop, calls=%fused_computation.15.clone.1 | loop fusion | flops 33554432 | bytes 4205568 | tf_op jit(solution)/shard_map/while/body/eval_jaxpr/convert_element_type | solution.py:110
  200.6 5.0 %convolution_add_fusion.4 = f32[72,8192]{1,0:T(8,128)} fusion(bf16[256,4096]{1,0:T(8,128)(2,1)} %get-tuple-element.410, bf16[256,4096]{1,0:T(8,128)(2,1)S(1)} %get-tuple-element.411, f32[72,8192]{1,0:T(8,128)} %get-tuple-element.435, pred[]{:T(512)S(6)} %compare.18, s32[72]{0:T(128)S(1)} %get-tuple-element.452, f32[256]{0:T(256)S(1)} %bitcast.227, ...), kind=kOutput, calls=%fused_computation.3.clone.1 | convolution fusion | flops 311871488 | bytes 8922401 | tf_op jit(solution)/shard_map/while/body/eval_jaxpr/dot_general | solution.py:115
  208.2 6.8 %multiply_convert_fusion.3 = (bf16[256,4096]{1,0:T(8,128)(2,1)S(1)}, bf16[256,4096]{1,0:T(8,128)(2,1)}) fusion(f32[256]{0:T(256)S(1)} %bitcast.217, f32[256]{0:T(256)S(1)} %bitcast.218, f32[256]{0:T(256)S(1)} %bitcast.219, f32[256]{0:T(256)S(1)} %bitcast.220, f32[256]{0:T(256)S(1)} %bitcast.221, f32[256]{0:T(256)S(1)} %bitcast.222, ...), kind=kLoop, calls=%fused_computation.15.clone.1 | loop fusion | flops 33554432 | bytes 4205568 | tf_op jit(solution)/shard_map/while/body/eval_jaxpr/convert_element_type | solution.py:110
  215.3 5.0 %convolution_add_fusion.4 = f32[72,8192]{1,0:T(8,128)} fusion(bf16[256,4096]{1,0:T(8,128)(2,1)} %get-tuple-element.410, bf16[256,4096]{1,0:T(8,128)(2,1)S(1)} %get-tuple-element.411, f32[72,8192]{1,0:T(8,128)} %get-tuple-element.435, pred[]{:T(512)S(6)} %compare.18, s32[72]{0:T(128)S(1)} %get-tuple-element.452, f32[256]{0:T(256)S(1)} %bitcast.227, ...), kind=kOutput, calls=%fused_computation.3.clone.1 | convolution fusion | flops 311871488 | bytes 8922401 | tf_op jit(solution)/shard_map/while/body/eval_jaxpr/dot_general | solution.py:115
  222.9 6.8 %multiply_convert_fusion.3 = (bf16[256,4096]{1,0:T(8,128)(2,1)S(1)}, bf16[256,4096]{1,0:T(8,128)(2,1)}) fusion(f32[256]{0:T(256)S(1)} %bitcast.217, f32[256]{0:T(256)S(1)} %bitcast.218, f32[256]{0:T(256)S(1)} %bitcast.219, f32[256]{0:T(256)S(1)} %bitcast.220, f32[256]{0:T(256)S(1)} %bitcast.221, f32[256]{0:T(256)S(1)} %bitcast.222, ...), kind=kLoop, calls=%fused_computation.15.clone.1 | loop fusion | flops 33554432 | bytes 4205568 | tf_op jit(solution)/shard_map/while/body/eval_jaxpr/convert_element_type | solution.py:110
  230.0 5.0 %convolution_add_fusion.4 = f32[72,8192]{1,0:T(8,128)} fusion(bf16[256,4096]{1,0:T(8,128)(2,1)} %get-tuple-element.410, bf16[256,4096]{1,0:T(8,128)(2,1)S(1)} %get-tuple-element.411, f32[72,8192]{1,0:T(8,128)} %get-tuple-element.435, pred[]{:T(512)S(6)} %compare.18, s32[72]{0:T(128)S(1)} %get-tuple-element.452, f32[256]{0:T(256)S(1)} %bitcast.227, ...), kind=kOutput, calls=%fused_computation.3.clone.1 | convolution fusion | flops 311871488 | bytes 8922401 | tf_op jit(solution)/shard_map/while/body/eval_jaxpr/dot_general | solution.py:115
  236.0 2.2 collective-permute-start
  238.2 1.6 slice.242
  239.8 11.9 %collective-permute-done = f32[8,8192]{1,0:T(8,128)S(1)} collective-permute-done((f32[8,8192]{1,0:T(8,128)S(1)}, f32[8,8192]{1,0:T(8,128)S(1)}, u32[]{:S(2)}, u32[]{:S(2)}) %collective-permute-start) | collective-permute-done | bytes 262176 | tf_op jit(solution)/shard_map/ppermute | solution.py:16
  252.7 1.5 pad_maximum_fusion
  254.1 5.4 %all-to-all-start = ((f32[4,16,8192]{2,1,0:T(8,128)}), f32[4,16,8192]{2,1,0:T(8,128)S(1)}, u32[]{:S(2)}, u32[]{:S(2)}) async-start(f32[4,16,8192]{2,1,0:T(8,128)} %bitcast.203), calls=%async_computation | async-start | bytes 4194304 | tf_op jit(solution)/shard_map/all_to_all | solution.py:26
  259.7 26.1 %all-to-all-done = f32[4,16,8192]{2,1,0:T(8,128)S(1)} async-done(((f32[4,16,8192]{2,1,0:T(8,128)}), f32[4,16,8192]{2,1,0:T(8,128)S(1)}, u32[]{:S(2)}, u32[]{:S(2)}) %all-to-all-start) | async-done | bytes 2097184 | tf_op jit(solution)/shard_map/all_to_all | solution.py:26
  289.5 1.8 fusion.56
  291.2 2.6 fusion.46
  293.8 1.7 copy.44
  297.0 7.2 %all-to-all-start.2 = ((f32[256,1,1,256]{3,2,1,0:T(1,128)}), f32[256,1,1,256]{3,2,1,0:T(1,128)S(1)}, u32[]{:S(2)}, u32[]{:S(2)}) async-start(f32[256,1,1,256]{3,2,1,0:T(1,128)} %reshape_transpose_transpose_reshape_reshape_reshape.9), calls=%async_computation.2 | async-start | bytes 524288 | tf_op jit(solution)/shard_map/all_to_all | solution.py:42
  304.2 1.8 fusion.58
  306.0 1.8 fusion.47
  309.9 9.8 %all-to-all-done.2 = f32[256,1,1,256]{3,2,1,0:T(1,128)S(1)} async-done(((f32[256,1,1,256]{3,2,1,0:T(1,128)}), f32[256,1,1,256]{3,2,1,0:T(1,128)S(1)}, u32[]{:S(2)}, u32[]{:S(2)}) %all-to-all-start.2) | async-done | bytes 262176 | tf_op jit(solution)/shard_map/all_to_all | solution.py:42
  319.7 5.4 %all-to-all-start.1 = ((f32[256,1,1,256]{3,2,1,0:T(1,128)}), f32[256,1,1,256]{3,2,1,0:T(1,128)S(1)}, u32[]{:S(2)}, u32[]{:S(2)}) async-start(f32[256,1,1,256]{3,2,1,0:T(1,128)} %reshape_transpose_transpose_reshape_reshape_reshape.8), calls=%async_computation.1 | async-start | bytes 524288 | tf_op jit(solution)/shard_map/all_to_all | solution.py:42
  327.1 13.7 %all-to-all-done.1 = f32[256,1,1,256]{3,2,1,0:T(1,128)S(1)} async-done(((f32[256,1,1,256]{3,2,1,0:T(1,128)}), f32[256,1,1,256]{3,2,1,0:T(1,128)S(1)}, u32[]{:S(2)}, u32[]{:S(2)}) %all-to-all-start.1) | async-done | bytes 262176 | tf_op jit(solution)/shard_map/all_to_all | solution.py:42
  (194 shorter events, 64.2 us)
Async XLA Ops:
  0.0 9.5 %copy-start = (f32[8,8]{1,0:T(8,128)S(1)}, f32[8,8]{1,0:T(8,128)}, u32[]{:S(2)}) copy-start(f32[8,8]{1,0:T(8,128)} %get-tuple-element.450) | copy-start | bytes 772 | tf_op jit(solution)/shard_map/while
  14.1 9.5 %copy-start = (f32[8,8]{1,0:T(8,128)S(1)}, f32[8,8]{1,0:T(8,128)}, u32[]{:S(2)}) copy-start(f32[8,8]{1,0:T(8,128)} %get-tuple-element.450) | copy-start | bytes 772 | tf_op jit(solution)/shard_map/while
  28.8 9.5 %copy-start = (f32[8,8]{1,0:T(8,128)S(1)}, f32[8,8]{1,0:T(8,128)}, u32[]{:S(2)}) copy-start(f32[8,8]{1,0:T(8,128)} %get-tuple-element.450) | copy-start | bytes 772 | tf_op jit(solution)/shard_map/while
  43.5 9.5 %copy-start = (f32[8,8]{1,0:T(8,128)S(1)}, f32[8,8]{1,0:T(8,128)}, u32[]{:S(2)}) copy-start(f32[8,8]{1,0:T(8,128)} %get-tuple-element.450) | copy-start | bytes 772 | tf_op jit(solution)/shard_map/while
  58.2 9.5 %copy-start = (f32[8,8]{1,0:T(8,128)S(1)}, f32[8,8]{1,0:T(8,128)}, u32[]{:S(2)}) copy-start(f32[8,8]{1,0:T(8,128)} %get-tuple-element.450) | copy-start | bytes 772 | tf_op jit(solution)/shard_map/while
  73.0 9.5 %copy-start = (f32[8,8]{1,0:T(8,128)S(1)}, f32[8,8]{1,0:T(8,128)}, u32[]{:S(2)}) copy-start(f32[8,8]{1,0:T(8,128)} %get-tuple-element.450) | copy-start | bytes 772 | tf_op jit(solution)/shard_map/while
  87.7 9.5 %copy-start = (f32[8,8]{1,0:T(8,128)S(1)}, f32[8,8]{1,0:T(8,128)}, u32[]{:S(2)}) copy-start(f32[8,8]{1,0:T(8,128)} %get-tuple-element.450) | copy-start | bytes 772 | tf_op jit(solution)/shard_map/while
  102.4 9.5 %copy-start = (f32[8,8]{1,0:T(8,128)S(1)}, f32[8,8]{1,0:T(8,128)}, u32[]{:S(2)}) copy-start(f32[8,8]{1,0:T(8,128)} %get-tuple-element.450) | copy-start | bytes 772 | tf_op jit(solution)/shard_map/while
  117.2 9.5 %copy-start = (f32[8,8]{1,0:T(8,128)S(1)}, f32[8,8]{1,0:T(8,128)}, u32[]{:S(2)}) copy-start(f32[8,8]{1,0:T(8,128)} %get-tuple-element.450) | copy-start | bytes 772 | tf_op jit(solution)/shard_map/while
  131.9 9.5 %copy-start = (f32[8,8]{1,0:T(8,128)S(1)}, f32[8,8]{1,0:T(8,128)}, u32[]{:S(2)}) copy-start(f32[8,8]{1,0:T(8,128)} %get-tuple-element.450) | copy-start | bytes 772 | tf_op jit(solution)/shard_map/while
  146.6 9.5 %copy-start = (f32[8,8]{1,0:T(8,128)S(1)}, f32[8,8]{1,0:T(8,128)}, u32[]{:S(2)}) copy-start(f32[8,8]{1,0:T(8,128)} %get-tuple-element.450) | copy-start | bytes 772 | tf_op jit(solution)/shard_map/while
  161.4 9.5 %copy-start = (f32[8,8]{1,0:T(8,128)S(1)}, f32[8,8]{1,0:T(8,128)}, u32[]{:S(2)}) copy-start(f32[8,8]{1,0:T(8,128)} %get-tuple-element.450) | copy-start | bytes 772 | tf_op jit(solution)/shard_map/while
  176.1 9.5 %copy-start = (f32[8,8]{1,0:T(8,128)S(1)}, f32[8,8]{1,0:T(8,128)}, u32[]{:S(2)}) copy-start(f32[8,8]{1,0:T(8,128)} %get-tuple-element.450) | copy-start | bytes 772 | tf_op jit(solution)/shard_map/while
  190.8 9.5 %copy-start = (f32[8,8]{1,0:T(8,128)S(1)}, f32[8,8]{1,0:T(8,128)}, u32[]{:S(2)}) copy-start(f32[8,8]{1,0:T(8,128)} %get-tuple-element.450) | copy-start | bytes 772 | tf_op jit(solution)/shard_map/while
  205.6 9.5 %copy-start = (f32[8,8]{1,0:T(8,128)S(1)}, f32[8,8]{1,0:T(8,128)}, u32[]{:S(2)}) copy-start(f32[8,8]{1,0:T(8,128)} %get-tuple-element.450) | copy-start | bytes 772 | tf_op jit(solution)/shard_map/while
  220.3 9.5 %copy-start = (f32[8,8]{1,0:T(8,128)S(1)}, f32[8,8]{1,0:T(8,128)}, u32[]{:S(2)}) copy-start(f32[8,8]{1,0:T(8,128)} %get-tuple-element.450) | copy-start | bytes 772 | tf_op jit(solution)/shard_map/while
  236.0 15.7 %collective-permute-start = (f32[8,8192]{1,0:T(8,128)S(1)}, f32[8,8192]{1,0:T(8,128)S(1)}, u32[]{:S(2)}, u32[]{:S(2)}) collective-permute-start(f32[8,8192]{1,0:T(8,128)S(1)} %slice.241), channel_id=1, source_target_pairs={{0,4},{4,8},{8,12},{12,16},{16,20},{20,24},{24,28},{28,32},{32,36}... | collective-permute-start | bytes 786440 | tf_op jit(solution)/shard_map/ppermute | solution.py:16
  254.1 31.6 %all-to-all-start = ((f32[4,16,8192]{2,1,0:T(8,128)}), f32[4,16,8192]{2,1,0:T(8,128)S(1)}, u32[]{:S(2)}, u32[]{:S(2)}) async-start(f32[4,16,8192]{2,1,0:T(8,128)} %bitcast.203), calls=%async_computation | async-start | bytes 4194304 | tf_op jit(solution)/shard_map/all_to_all | solution.py:26
  297.0 22.8 %all-to-all-start.2 = ((f32[256,1,1,256]{3,2,1,0:T(1,128)}), f32[256,1,1,256]{3,2,1,0:T(1,128)S(1)}, u32[]{:S(2)}, u32[]{:S(2)}) async-start(f32[256,1,1,256]{3,2,1,0:T(1,128)} %reshape_transpose_transpose_reshape_reshape_reshape.9), calls=%async_computation.2 | async-start | bytes 524288 | tf_op jit(solution)/shard_map/all_to_all | solution.py:42
  319.7 21.1 %all-to-all-start.1 = ((f32[256,1,1,256]{3,2,1,0:T(1,128)}), f32[256,1,1,256]{3,2,1,0:T(1,128)S(1)}, u32[]{:S(2)}, u32[]{:S(2)}) async-start(f32[256,1,1,256]{3,2,1,0:T(1,128)} %reshape_transpose_transpose_reshape_reshape_reshape.8), calls=%async_computation.1 | async-start | bytes 524288 | tf_op jit(solution)/shard_map/all_to_all | solution.py:42
where the time goes:
time: 349 us; the launch traced here: 347 us
  other arithmetic  126 us (36%)
  matrix products  114 us (33%)
  waiting for transfers between devices  61.5 us (18%)
  local copies, waits for them, and re-layouts  24.8 us (7%)
  starting transfers between devices  20.3 us (6%)
    convert_element_type x16, other arithmetic, add_block(): (vis_now[0][:, None] * col_weight).astype(jnp.bfloat16)  109 us
    dot_general x16, matrix products, add_block(): lax.dot_general(row_weight, col_values, (((0,), (0,)), ((), ())), preferr...  78.9 us
    all_to_all x1, waiting for transfers between devices, sent_and_summed(): lax.all_to_all(tiles, axis, split_axis=0, concat_axis=0, tiled=True)  26.1 us
    all_to_all x2, waiting for transfers between devices, one_exchange(): tiles = lax.all_to_all(tiles, axis, split_axis=0, concat_axis=0, tiled=True)  23.6 us
    dot_general x32, matrix products, lookup(): return jnp.dot(one_hot, kernel, precision=lax.Precision.HIGHEST)  17.6 us
    dot_general x12, matrix products, product(): jnp.einsum(pattern, left_one, right_one, precision=lax.Precision.HIGHEST)  14.2 us
    slice x16, local copies, waits for them, and re-layouts, add_block(): vis_now[0][:, None] * col_weight  13.4 us
    mul x16, other arithmetic, add_block(): row_start = tap_count * tiles_now[0] + offsets_now[0]  13.3 us
  transfers between devices with their start and end apart: 4, of which 4 were waited for; matrix products, arithmetic and copies ran while one was open for 3% of the time, Pallas kernels for 0%

commit v1 on v0

v1 whole, which is shorter than its diff:
```python
import functools

import jax
import jax.numpy as jnp
import numpy as np
from jax import lax
from jax.experimental import pallas as pl
from jax.experimental.pallas import tpu as pltpu
from jax.sharding import PartitionSpec as P

G = 4096
MESH = pl.DeviceIdType.MESH
BF16 = jnp.bfloat16
F32 = jnp.float32
CHUNK = 512
N_VIS = 4096
ROWS_W = 272
ROWS_S = 48


def split_table(x):
    hi = x.astype(np.float32).astype(jnp.dtype(BF16))
    return hi, (x - hi.astype(np.float64)).astype(np.float32).astype(jnp.dtype(BF16))


def unit(turns):
    angle = 2.0 * np.pi * (turns % 1.0)
    return np.cos(angle), np.sin(angle)


@functools.cache
def tables_v():
    h = np.arange(16)
    er, ei = unit(h[:, None] * h[None, :] / 16)
    d = np.concatenate([np.kron(np.eye(16), er), np.kron(np.eye(16), ei)], axis=1)
    w, lane = np.arange(ROWS_W), np.arange(128)
    tr, ti = unit(w[:, None] * (lane % 16)[None, :] / 4096)
    tw = np.stack([tr, ti]).astype(np.float32) / np.float32(G)
    q = np.arange(256)
    wr, wi = unit(q[:, None] * q[None, :] / 256)
    big = np.block([[wr, -wi], [wi, wr]])
    return split_table(d) + (tw,) + split_table(big)


@functools.cache
def tables_u():
    k, s = np.arange(128), np.arange(64)
    er, ei = unit(k[:, None] * s[None, :] / 64)
    e = np.block([[er, -ei], [ei, er]])
    lane = np.arange(128)
    tr, ti = unit(k[:, None] * (lane // 16)[None, :] / 512)
    tw1 = np.stack([tr, ti]).astype(np.float32)
    row = np.arange(64)
    dr, di = unit((row // 16)[:, None] * (lane // 16)[None, :] / 4)
    same = (row % 16)[:, None] == (lane % 16)[None, :]
    d = np.concatenate([dr * same, di * same], axis=0)
    j, k1 = np.arange(8), np.arange(4)
    ar, ai = unit(j[:, None, None] * (k[None, None, :] + 128 * k1[None, :, None]) / 4096)
    tw2 = np.stack([ar.reshape(32, 128), ai.reshape(32, 128)]).astype(np.float32)
    return split_table(e) + (tw1,) + split_table(d) + (tw2,)


def halves(x):
    hi = x.astype(BF16)
    return hi, (x - hi.astype(F32)).astype(BF16)


def dot(a, b, dims):
    return lax.dot_general(a, b, (dims, ((), ())), preferred_element_type=F32)


def dot3(a, b, dims):
    return dot(a[0], b[0], dims) + (dot(a[1], b[0], dims) + dot(a[0], b[1], dims))


NN = ((1,), (0,))
NT = ((1,), (1,))


def build_tables(kern_ref, g, tab_ref):
    sub = lax.broadcasted_iota(jnp.int32, (8, 128), 0)
    for o in range(8):
        col = jnp.zeros((8, 128), F32)
        row = jnp.zeros((8, 128), F32)
        for j in range(8):
            col = jnp.where(sub == j, kern_ref[o, (j - o) % 8], col)
            row = jnp.where(sub == j, kern_ref[o, lax.rem(g + (j - o) % 8, 8)], row)
        tab_ref[o] = col
        tab_ref[8 + o] = row.astype(BF16).astype(F32)


def pick(which, tab_ref, first):
    out = jnp.zeros((8, 128), F32)
    for o in range(8):
        out = jnp.where(which == o, tab_ref[first + o], out)
    return out


def build(vis_ref, tile_ref, off_ref, start, slab, g, tab_ref, parts):
    bt, at, sa, sb = parts
    sub8 = lax.broadcasted_iota(jnp.int32, (8, 128), 0)
    sub16 = lax.broadcasted_iota(jnp.int32, (16, 128), 0)
    half = sub16 // 8
    zero = jnp.zeros((16, 128), BF16)

    def wide(x, rows):
        return jnp.broadcast_to(x, (rows, 128))

    def as_bf16(x):
        return x.astype(F32).astype(BF16)

    for q in range(CHUNK // 128):
        here = pl.ds(start + q * 128, 128)
        lanes = slice(q * 128, (q + 1) * 128)
        tile_row = tile_ref[0:1, here] - 8 * slab
        tile_col = tile_ref[1:2, here]
        off_row = off_ref[0:1, here]
        off_col = off_ref[1:2, here]
        if bt is not None or sb is not None:
            taps = pick(wide(off_col, 8), tab_ref, 0)
            wrapped = (sub8 < off_col).astype(jnp.int32)
            carry = jnp.concatenate([wrapped, wrapped], axis=0) - half
            values = []
            for c in range(2):
                one = vis_ref[c : c + 1, here] * taps
                values.append(jnp.concatenate([one, one], axis=0).astype(BF16))
        if bt is not None:
            need = as_bf16(carry + (tile_col & 31))
            for m in range(17):
                hit = need == BF16(2 * m)
                for c in range(2):
                    bt[c * ROWS_W + 16 * m : c * ROWS_W + 16 * m + 16, lanes] = jnp.where(hit, values[c], zero)
        if sb is not None:
            need = as_bf16(carry + (tile_col & 3))
            for m in range(3):
                hit = need == BF16(2 * m)
                for c in range(2):
                    sb[c * ROWS_S + 16 * m : c * ROWS_S + 16 * m + 16, lanes] = jnp.where(hit, values[c], zero)
        if at is not None or sa is not None:
            row_taps = pick(wide(off_row, 8), tab_ref, 8)
            own_h = sub16 == wide(tile_col >> 5, 16)
            fine = (tile_col >> 2) & 7
            for b in range(2):
                spread = jnp.where(own_h, wide(row_taps[4 * b : 4 * b + 1], 16), 0.0).astype(BF16)
                row_tile = tile_row + (4 * b + g < off_row).astype(jnp.int32)
                if at is not None:
                    need = as_bf16(wide(row_tile, 16))
                    for t in range(8):
                        first = b * 128 + t * 16
                        at[first : first + 16, lanes] = jnp.where(need == BF16(t), spread, zero)
                if sa is not None:
                    need = as_bf16(wide(jnp.where(row_tile == 8, fine, -1), 16))
                    for t in range(8):
                        first = b * 128 + t * 16
                        sa[first : first + 16, lanes] = jnp.where(need == BF16(t), spread, zero)


def grid_block(vis_ref, tile_ref, off_ref, slab, g, tab_ref, scratch, main, spill):
    bt, at, sa, sb, acc, accs = scratch

    def step(i, _):
        start = pl.multiple_of(i * CHUNK, CHUNK)
        parts = (bt if main else None, at if main else None, sa if spill else None, sb if spill else None)
        build(vis_ref, tile_ref, off_ref, start, slab, g, tab_ref, parts)
        if main:
            acc[...] += dot(bt[...], at[...], NT)
        if spill:
            accs[...] += dot(sa[...], sb[...], NT)
        return 0

    lax.fori_loop(0, N_VIS // CHUNK, step, 0)


def add_spill(acc, got):
    for c in range(2):
        for b in range(2):
            for f in range(8):
                rows = pl.ds(c * ROWS_W + 32 * f, ROWS_S)
                acc[rows, b * 128 : b * 128 + 16] += got[
                    c * ROWS_S : (c + 1) * ROWS_S, b * 128 + f * 16 : b * 128 + f * 16 + 16
                ]


def row_transform(acc, d_hi, d_lo, tw, w_hi, w_lo, out_ref):
    n = ROWS_W
    p = dot3(halves(acc[...]), (d_hi[...], d_lo[...]), NN)
    real = p[:n, :256] - p[n:, 256:]
    imag = p[:n, 256:] + p[n:, :256]
    cos = jnp.concatenate([tw[0], tw[0]], axis=1)
    sin = jnp.concatenate([tw[1], tw[1]], axis=1)
    turned = (real * cos - imag * sin, real * sin + imag * cos)
    both = jnp.concatenate([jnp.concatenate([t[:16] + t[256:], t[16:256]], axis=0) for t in turned], axis=0)
    s = dot3((w_hi[...], w_lo[...]), halves(both), NN)
    for c in range(2):
        for b in range(2):
            out_ref[pl.ds(2 * c + b, 256, stride=4), :] = s[c * 256 : (c + 1) * 256, b * 128 : (b + 1) * 128]


def grid_kernel(
    vis, tiles, offs, kern, d_hi, d_lo, tw, w_hi, w_lo, out_ref,
    got_vis, got_tiles, got_offs, tab, bt, at, sa, sb, acc, accs, spill_out, spill_in,
    send_sems, recv_sems, spill_sems,
):
    slab, g = lax.axis_index("rows"), lax.axis_index("grp")
    slabs = lax.axis_size("rows")
    after, before = lax.rem(slab + 1, slabs), lax.rem(slab + slabs - 1, slabs)
    low = lax.rem(g, 2)
    sibling = g + 1 - 2 * low
    across = lax.rem(g + 2, 4)

    barrier = pltpu.get_barrier_semaphore()
    for peer in ((slab, sibling), (slab, across), (after, g), (before, g)):
        pl.semaphore_signal(barrier, inc=1, device_id=peer, device_id_type=MESH)

    build_tables(kern, g, tab)
    acc[...] = jnp.zeros_like(acc)
    accs[...] = jnp.zeros_like(accs)
    pl.semaphore_wait(barrier, 4)

    def send(sources, slot, peer):
        copies = []
        for n, (source, target) in enumerate(zip(sources, (got_vis, got_tiles, got_offs))):
            copies.append(
                pltpu.make_async_remote_copy(
                    src_ref=source,
                    dst_ref=target.at[slot],
                    send_sem=send_sems.at[slot, n],
                    recv_sem=recv_sems.at[slot, n],
                    device_id=(slab, peer),
                    device_id_type=MESH,
                )
            )
        for copy in copies:
            copy.start()
        return copies

    own = (vis, tiles, offs)
    held = [own] + [(got_vis.at[n], got_tiles.at[n], got_offs.at[n]) for n in range(3)]
    to_across = send(own, 1, across)
    to_sibling = send(own, 0, sibling)
    scratch = (bt, at, sa, sb, acc, accs)

    def block(n, main, spill):
        grid_block(*held[n], slab, g, tab, scratch, main, spill)

    block(0, True, True)
    for copy in to_sibling:
        copy.wait_recv()
    block(1, True, True)
    for copy in to_across:
        copy.wait_recv()
    relayed = send(held[2], 2, sibling)
    block(2, False, True)
    for copy in relayed:
        copy.wait_recv()
    block(3, False, True)
    spill_out[...] = accs[...].T
    spill_copy = pltpu.make_async_remote_copy(
        src_ref=spill_out,
        dst_ref=spill_in,
        send_sem=spill_sems.at[0],
        recv_sem=spill_sems.at[1],
        device_id=(after, g),
        device_id_type=MESH,
    )
    spill_copy.start()
    block(2, True, False)
    block(3, True, False)
    spill_copy.wait_recv()
    add_spill(acc, spill_in)
    row_transform(acc, d_hi, d_lo, tw, w_hi, w_lo, out_ref)
    for copy in to_sibling + to_across + relayed + [spill_copy]:
        copy.wait_send()


def vmem(shape, dtype):
    return pltpu.VMEM(shape, dtype)


def grid_scratch():
    return [
        vmem((16, 8, 128), F32),
        vmem((2 * ROWS_W, CHUNK), BF16),
        vmem((256, CHUNK), BF16),
        vmem((256, CHUNK), BF16),
        vmem((2 * ROWS_S, CHUNK), BF16),
        vmem((2 * ROWS_W, 256), F32),
        vmem((256, 2 * ROWS_S), F32),
        vmem((2 * ROWS_S, 256), F32),
        vmem((2 * ROWS_S, 256), F32),
    ]


def row_stage(visibilities, uv_tiles, kernel_offsets, kernel):
    in_vmem = pl.BlockSpec(memory_space=pltpu.VMEM)
    return pl.pallas_call(
        grid_kernel,
        out_shape=jax.ShapeDtypeStruct((1024, 128), F32),
        in_specs=[in_vmem] * 3 + [pl.BlockSpec(memory_space=pltpu.SMEM)] + [in_vmem] * 5,
        out_specs=in_vmem,
        scratch_shapes=[
            vmem((3, 2, N_VIS), F32),
            vmem((3, 2, N_VIS), jnp.int32),
            vmem((3, 2, N_VIS), jnp.int32),
        ]
        + grid_scratch()
        + [
            pltpu.SemaphoreType.DMA((3, 3)),
            pltpu.SemaphoreType.DMA((3, 3)),
            pltpu.SemaphoreType.DMA((2,)),
        ],
        compiler_params=pltpu.CompilerParams(
            collective_id=0, has_side_effects=True, vmem_limit_bytes=50 * 2**20
        ),
        name="grid_rows",
    )(visibilities, uv_tiles, kernel_offsets, kernel, *tables_v())


def fft8(x):
    def add(a, b):
        return (a[0] + b[0], a[1] + b[1])

    def sub(a, b):
        return (a[0] - b[0], a[1] - b[1])

    def by_i(a):
        return (-a[1], a[0])

    def fft4(a):
        s, d = add(a[0], a[2]), sub(a[0], a[2])
        t, e = add(a[1], a[3]), by_i(sub(a[1], a[3]))
        return [add(s, t), add(d, e), sub(s, t), sub(d, e)]

    root = np.float32(np.sqrt(0.5))
    even, odd = fft4(x[0::2]), fft4(x[1::2])
    one, three = odd[1], odd[3]
    odd[1] = (root * (one[0] - one[1]), root * (one[0] + one[1]))
    odd[2] = by_i(odd[2])
    odd[3] = (root * (-three[0] - three[1]), root * (three[0] - three[1]))
    return [add(even[k], odd[k]) for k in range(4)] + [sub(even[k], odd[k]) for k in range(4)]


def column_kernel(r_ref, e_hi, e_lo, tw1, d_hi, d_lo, tw2, out_ref):
    sums = []
    for j in range(8):
        b, g = divmod(j, 4)
        x = jnp.concatenate([r_ref[pl.ds(4 * g + 2 * c + b, 64, stride=16), :] for c in range(2)], axis=0)
        z = dot3((e_hi[...], e_lo[...]), halves(x), NN)
        real, imag = z[:128], z[128:]
        cos, sin = tw1[0], tw1[1]
        turned = jnp.concatenate([real * cos - imag * sin, real * sin + imag * cos], axis=0)
        p = dot3((d_hi[...], d_lo[...]), halves(turned), NT)
        real = p[:64, :128] - p[64:, 128:]
        imag = p[:64, 128:] + p[64:, :128]
        cos = jnp.concatenate([jnp.broadcast_to(tw2[0, 4 * j + k : 4 * j + k + 1], (16, 128)) for k in range(4)], axis=0)
        sin = jnp.concatenate([jnp.broadcast_to(tw2[1, 4 * j + k : 4 * j + k + 1], (16, 128)) for k in range(4)], axis=0)
        sums.append((real * cos - imag * sin, real * sin + imag * cos))
    for k2, pair in enumerate(fft8(sums)):
        for c in range(2):
            for k1 in range(4):
                first = 512 * k2 + 128 * k1
                out_ref[c, :, first : first + 128] = pair[c][16 * k1 : 16 * k1 + 16]


def column_stage(received):
    return pl.pallas_call(
        column_kernel,
        out_shape=jax.ShapeDtypeStruct((2, 16, G), F32),
        in_specs=[pl.BlockSpec(memory_space=pltpu.VMEM)] * 7,
        out_specs=pl.BlockSpec(memory_space=pltpu.VMEM),
        compiler_params=pltpu.CompilerParams(vmem_limit_bytes=40 * 2**20),
        name="columns",
    )(received, *tables_u())


def shards(visibilities, uv_tiles, kernel_offsets, kernel):
    blocks = row_stage(visibilities, uv_tiles, kernel_offsets, kernel)
    received = lax.all_to_all(
        blocks.reshape(256, 4, 128), ("rows", "grp"), split_axis=0, concat_axis=0, tiled=True
    )
    return column_stage(received.reshape(1024, 128))


def solution(mesh):
    in_specs = (P(None, ("rows", "grp")), P(None, ("rows", "grp")), P(None, ("rows", "grp")), P())
    out_specs = P(None, ("rows", "grp"), None)
    return jax.shard_map(shards, mesh=mesh, in_specs=in_specs, out_specs=out_specs, check_vma=False)
```

time: 349 us -> 69.4 us (0.20)
  other arithmetic: 126 us -> 0 us
  matrix products: 114 us -> 0 us
  waiting for transfers between devices: 61.5 us -> 0 us
  Pallas kernels: 0 us -> 33.7 us
  blocking collectives: 0 us -> 27.1 us
  starting transfers between devices: 20.3 us -> 0 us
  local copies, waits for them, and re-layouts: 24.8 us -> 7.94 us
    dot_general x60 -> x0, matrix products: 111 us -> none  [the longest x16 78.9 us: add_block(): lax.dot_general(row_weight, col_values, (((0,), (0,)), ((), ())), preferr...]
    convert_element_type x16 -> x0, other arithmetic: 109 us -> none  [add_block(): (vis_now[0][:, None] * col_weight).astype(jnp.bfloat16)]
    all_to_all x3 -> x0, waiting for transfers between devices: 49.6 us -> none  [the longest x1 26.1 us: sent_and_summed(): lax.all_to_all(tiles, axis, split_axis=0, concat_axis=0, tiled=True)]
    pallas_call x0 -> x2, Pallas kernels: none -> 33.7 us  [the longest x1 31.6 us: row_stage(): pl.pallas_call(grid_kernel, out_shape=jax.ShapeDtypeStruct((1024, 128), F...]
    all_to_all x0 -> x1, blocking collectives: none -> 27.1 us  [shards(): lax.all_to_all(blocks.reshape(256, 4, 128), ('rows', 'grp'), split_axis=0...]
    slice x51 -> x0, local copies, waits for them, and re-layouts: 18.2 us -> none  [the longest x16 13.4 us: add_block(): vis_now[0][:, None] * col_weight]
    all_to_all x3 -> x0, starting transfers between devices: 18.1 us -> none  [the longest x2 12.7 us: one_exchange(): tiles = lax.all_to_all(tiles, axis, split_axis=0, concat_axis=0, tiled=True)]
    mul x16 -> x0, other arithmetic: 13.3 us -> none  [add_block(): row_start = tap_count * tiles_now[0] + offsets_now[0]]
  transfers between devices with their start and end apart: 4 -> 0, of which waited for: 4 -> 0; matrix products, arithmetic and copies ran while one was open for 3% -> 0% of each run, Pallas kernels for 0% -> 0%
where the time goes in v1:
time: 69.4 us; the launch traced here: 68.8 us
  Pallas kernels  33.7 us (49%)
  blocking collectives  27.1 us (39%)
  local copies, waits for them, and re-layouts  7.94 us (11%)
    pallas_call x1, Pallas kernels, row_stage(): pl.pallas_call(grid_kernel, out_shape=jax.ShapeDtypeStruct((1024, 128), F...  31.6 us
    all_to_all x1, blocking collectives, shards(): lax.all_to_all(blocks.reshape(256, 4, 128), ('rows', 'grp'), split_axis=0...  27.1 us
    unnamed x30, local copies, waits for them, and re-layouts  7.94 us
    pallas_call x1, Pallas kernels, column_stage(): pl.pallas_call(column_kernel, out_shape=jax.ShapeDtypeStruct((2, 16, G),...  2.07 us

profile of v1, /device:TPU:1, one launch (start us, length us, event | category | flops | bytes accessed | tf_op | source)
XLA Modules:
  0.0 68.8 jit_solution(2185448616771028185)
XLA Ops:
  0.0 0.0 copy-start
  0.0 1.0 %copy-done = bf16[512,512]{1,0:T(8,128)(2,1)S(1)} copy-done((bf16[512,512]{1,0:T(8,128)(2,1)S(1)}, bf16[512,512]{1,0:T(8,128)(2,1)}, u32[]{:S(2)}) %copy-start) | copy-done | bytes 524312
  1.0 0.0 copy-start.1
  1.0 1.0 %copy-done.1 = bf16[512,512]{1,0:T(8,128)(2,1)S(1)} copy-done((bf16[512,512]{1,0:T(8,128)(2,1)S(1)}, bf16[512,512]{1,0:T(8,128)(2,1)}, u32[]{:S(2)}) %copy-start.1) | copy-done | bytes 524312
  2.1 0.0 copy-start.2
  2.1 1.0 %copy-done.2 = f32[2,272,128]{2,1,0:T(8,128)S(1)} copy-done((f32[2,272,128]{2,1,0:T(8,128)S(1)}, f32[2,272,128]{2,1,0:T(8,128)}, u32[]{:S(2)}) %copy-start.2) | copy-done | bytes 278552
  3.0 0.0 copy-start.3
  3.0 0.9 %copy-done.3 = bf16[256,512]{1,0:T(8,128)(2,1)S(1)} copy-done((bf16[256,512]{1,0:T(8,128)(2,1)S(1)}, bf16[256,512]{1,0:T(8,128)(2,1)}, u32[]{:S(2)}) %copy-start.3) | copy-done | bytes 262168
  4.0 0.0 copy-start.4
  4.0 0.9 %copy-done.4 = bf16[256,512]{1,0:T(8,128)(2,1)S(1)} copy-done((bf16[256,512]{1,0:T(8,128)(2,1)S(1)}, bf16[256,512]{1,0:T(8,128)(2,1)}, u32[]{:S(2)}) %copy-start.4) | copy-done | bytes 262168
  4.9 0.0 copy-start.8
  4.9 0.8 %copy-done.8 = f32[2,4096]{1,0:T(2,128)S(1)} copy-done((f32[2,4096]{1,0:T(2,128)S(1)}, f32[2,4096]{1,0:T(2,128)}, u32[]{:S(2)}) %copy-start.8) | copy-done | bytes 32792
  5.7 0.0 copy-start.9
  5.7 0.8 %copy-done.9 = s32[2,4096]{1,0:T(2,128)S(1)} copy-done((s32[2,4096]{1,0:T(2,128)S(1)}, s32[2,4096]{1,0:T(2,128)}, u32[]{:S(2)}) %copy-start.9) | copy-done | bytes 32792
  6.5 0.0 copy-start.10
  6.5 0.8 %copy-done.10 = s32[2,4096]{1,0:T(2,128)S(1)} copy-done((s32[2,4096]{1,0:T(2,128)S(1)}, s32[2,4096]{1,0:T(2,128)}, u32[]{:S(2)}) %copy-start.10) | copy-done | bytes 32792
  7.2 0.0 copy-start.14
  7.2 0.7 copy-done.14
  7.9 31.6 %grid_rows.1 = f32[1024,128]{1,0:T(8,128)S(1)} custom-call(f32[2,4096]{1,0:T(2,128)S(1)} %copy-done.8, s32[2,4096]{1,0:T(2,128)S(1)} %copy-done.9, s32[2,4096]{1,0:T(2,128)S(1)} %copy-done.10, f32[8,8]{1,0:T(8,128)S(1)} %copy-done.14, bf16[256,512]{1,0:T(8,128)(2,1)S(1)} %copy-done.4, bf16[256,512]{1,0:T(8,128)(2,1)S(1)} %copy-done.3, ...), custom_call_target="tpu_custom_call" | custom-call | tf_op jit(solution)/shard_map/grid_rows/pallas_call | solution.py:296
  39.5 0.0 copy-start.5
  39.5 0.0 copy-start.6
  39.5 0.0 copy-start.7
  39.5 0.0 copy-start.11
  39.5 0.0 copy-start.12
  39.6 0.0 copy-start.13
  39.6 27.1 %all_to_all.5 = f32[256,4,128]{2,1,0:T(4,128)S(1)} all-to-all(f32[256,4,128]{2,1,0:T(4,128)S(1)} %bitcast.2), channel_id=1, replica_groups=mesh['rows'=64,'grp'=4] {'rows','grp'}, dimensions={0} | all-to-all | bytes 1048576 | tf_op jit(solution)/shard_map/all_to_all | solution.py:378
  66.7 0.0 copy-done.5
  66.7 0.0 copy-done.6
  66.7 0.0 copy-done.7
  66.7 0.0 copy-done.11
  66.7 0.0 copy-done.12
  66.7 0.0 copy-done.13
  66.7 2.1 %columns.1 = f32[2,16,4096]{2,1,0:T(8,128)} custom-call(f32[1024,128]{1,0:T(8,128)S(1)} %bitcast.3, bf16[256,128]{1,0:T(8,128)(2,1)S(1)} %copy-done.7, bf16[256,128]{1,0:T(8,128)(2,1)S(1)} %copy-done.6, f32[2,128,128]{2,1,0:T(8,128)S(1)} %copy-done.5, bf16[128,128]{1,0:T(8,128)(2,1)S(1)} %copy-done.13, bf16[128,128]{1,0:T(8,128)(2,1)S(1)} %copy-done.12, ...), custom_call_target="tpu_custom_call" | custom-call | tf_op jit(solution)/shard_map/columns/pallas_call | solution.py:366
Async XLA Ops:
  0.0 1.0 %copy-start = (bf16[512,512]{1,0:T(8,128)(2,1)S(1)}, bf16[512,512]{1,0:T(8,128)(2,1)}, u32[]{:S(2)}) copy-start(bf16[512,512]{1,0:T(8,128)(2,1)} %constant.26.clone.w_lo) | copy-start | bytes 1572868
  1.0 1.0 %copy-start.1 = (bf16[512,512]{1,0:T(8,128)(2,1)S(1)}, bf16[512,512]{1,0:T(8,128)(2,1)}, u32[]{:S(2)}) copy-start(bf16[512,512]{1,0:T(8,128)(2,1)} %constant.25.clone.w_hi) | copy-start | bytes 1572868
  2.1 1.0 %copy-start.2 = (f32[2,272,128]{2,1,0:T(8,128)S(1)}, f32[2,272,128]{2,1,0:T(8,128)}, u32[]{:S(2)}) copy-start(f32[2,272,128]{2,1,0:T(8,128)} %constant.24.clone.tw) | copy-start | bytes 835588
  3.0 0.9 %copy-start.3 = (bf16[256,512]{1,0:T(8,128)(2,1)S(1)}, bf16[256,512]{1,0:T(8,128)(2,1)}, u32[]{:S(2)}) copy-start(bf16[256,512]{1,0:T(8,128)(2,1)} %constant.23.clone.d_lo) | copy-start | bytes 786436
  4.0 0.9 %copy-start.4 = (bf16[256,512]{1,0:T(8,128)(2,1)S(1)}, bf16[256,512]{1,0:T(8,128)(2,1)}, u32[]{:S(2)}) copy-start(bf16[256,512]{1,0:T(8,128)(2,1)} %constant.22.clone.d_hi) | copy-start | bytes 786436
  4.9 0.8 %copy-start.8 = (f32[2,4096]{1,0:T(2,128)S(1)}, f32[2,4096]{1,0:T(2,128)}, u32[]{:S(2)}) copy-start(f32[2,4096]{1,0:T(2,128)} %vis.1) | copy-start | bytes 98308
  5.7 0.8 %copy-start.9 = (s32[2,4096]{1,0:T(2,128)S(1)}, s32[2,4096]{1,0:T(2,128)}, u32[]{:S(2)}) copy-start(s32[2,4096]{1,0:T(2,128)} %tiles.1) | copy-start | bytes 98308
  6.5 0.8 %copy-start.10 = (s32[2,4096]{1,0:T(2,128)S(1)}, s32[2,4096]{1,0:T(2,128)}, u32[]{:S(2)}) copy-start(s32[2,4096]{1,0:T(2,128)} %offs.1) | copy-start | bytes 98308
  7.2 0.7 copy-start.14
  39.5 27.2 %copy-start.5 = (f32[2,128,128]{2,1,0:T(8,128)S(1)}, f32[2,128,128]{2,1,0:T(8,128)}, u32[]{:S(2)}) copy-start(f32[2,128,128]{2,1,0:T(8,128)} %constant.29.clone.tw1) | copy-start | bytes 393220
  39.5 27.2 %copy-start.6 = (bf16[256,128]{1,0:T(8,128)(2,1)S(1)}, bf16[256,128]{1,0:T(8,128)(2,1)}, u32[]{:S(2)}) copy-start(bf16[256,128]{1,0:T(8,128)(2,1)} %constant.28.clone.e_lo) | copy-start | bytes 196612
  39.5 27.2 %copy-start.7 = (bf16[256,128]{1,0:T(8,128)(2,1)S(1)}, bf16[256,128]{1,0:T(8,128)(2,1)}, u32[]{:S(2)}) copy-start(bf16[256,128]{1,0:T(8,128)(2,1)} %constant.27.clone.e_hi) | copy-start | bytes 196612
  39.5 27.2 %copy-start.11 = (f32[2,32,128]{2,1,0:T(8,128)S(1)}, f32[2,32,128]{2,1,0:T(8,128)}, u32[]{:S(2)}) copy-start(f32[2,32,128]{2,1,0:T(8,128)} %constant.32.clone.tw2) | copy-start | bytes 98308
  39.5 27.2 %copy-start.12 = (bf16[128,128]{1,0:T(8,128)(2,1)S(1)}, bf16[128,128]{1,0:T(8,128)(2,1)}, u32[]{:S(2)}) copy-start(bf16[128,128]{1,0:T(8,128)(2,1)} %constant.31.clone.d_lo) | copy-start | bytes 98308
  39.6 27.2 %copy-start.13 = (bf16[128,128]{1,0:T(8,128)(2,1)S(1)}, bf16[128,128]{1,0:T(8,128)(2,1)}, u32[]{:S(2)}) copy-start(bf16[128,128]{1,0:T(8,128)(2,1)} %constant.30.clone.d_hi) | copy-start | bytes 98308

commit v2 on v1

--- a/solution.py
+++ b/solution.py
@@ -12,7 +12,7 @@
 MESH = pl.DeviceIdType.MESH
 BF16 = jnp.bfloat16
 F32 = jnp.float32
-CHUNK = 512
+CHUNK = 1024
 N_VIS = 4096
 ROWS_W = 272
 ROWS_S = 48
@@ -193,31 +193,99 @@
     s = dot3((w_hi[...], w_lo[...]), halves(both), NN)
     for c in range(2):
         for b in range(2):
-            out_ref[pl.ds(2 * c + b, 256, stride=4), :] = s[c * 256 : (c + 1) * 256, b * 128 : (b + 1) * 128]
-
-
-def grid_kernel(
-    vis, tiles, offs, kern, d_hi, d_lo, tw, w_hi, w_lo, out_ref,
-    got_vis, got_tiles, got_offs, tab, bt, at, sa, sb, acc, accs, spill_out, spill_in,
-    send_sems, recv_sems, spill_sems,
-):
+            out_ref[:, 2 * c + b, :] = s[c * 256 : (c + 1) * 256, b * 128 : (b + 1) * 128]
+
+
+def fft8(x):
+    def add(a, b):
+        return (a[0] + b[0], a[1] + b[1])
+
+    def sub(a, b):
+        return (a[0] - b[0], a[1] - b[1])
+
+    def by_i(a):
+        return (-a[1], a[0])
+
+    def fft4(a):
+        s, d = add(a[0], a[2]), sub(a[0], a[2])
+        t, e = add(a[1], a[3]), by_i(sub(a[1], a[3]))
+        return [add(s, t), add(d, e), sub(s, t), sub(d, e)]
+
+    root = np.float32(np.sqrt(0.5))
+    even, odd = fft4(x[0::2]), fft4(x[1::2])
+    one, three = odd[1], odd[3]
+    odd[1] = (root * (one[0] - one[1]), root * (one[0] + one[1]))
+    odd[2] = by_i(odd[2])
+    odd[3] = (root * (-three[0] - three[1]), root * (three[0] - three[1]))
+    return [add(even[k], odd[k]) for k in range(4)] + [sub(even[k], odd[k]) for k in range(4)]
+
+
+def column_transform(r_ref, e_hi, e_lo, tw1, d_hi, d_lo, tw2, out_ref):
+    sums = []
+    for j in range(8):
+        b, g = divmod(j, 4)
+        x = jnp.concatenate([r_ref[pl.ds(g, 64, stride=4), 2 * c + b, :] for c in range(2)], axis=0)
+        z = dot3((e_hi[...], e_lo[...]), halves(x), NN)
+        real, imag = z[:128], z[128:]
+        cos, sin = tw1[0], tw1[1]
+        turned = jnp.concatenate([real * cos - imag * sin, real * sin + imag * cos], axis=0)
+        p = dot3((d_hi[...], d_lo[...]), halves(turned), NT)
+        real = p[:64, :128] - p[64:, 128:]
+        imag = p[:64, 128:] + p[64:, :128]
+        cos = jnp.concatenate([jnp.broadcast_to(tw2[0, 4 * j + k : 4 * j + k + 1], (16, 128)) for k in range(4)], axis=0)
+        sin = jnp.concatenate([jnp.broadcast_to(tw2[1, 4 * j + k : 4 * j + k + 1], (16, 128)) for k in range(4)], axis=0)
+        sums.append((real * cos - imag * sin, real * sin + imag * cos))
+    for k2, pair in enumerate(fft8(sums)):
+        for c in range(2):
+            for k1 in range(4):
+                first = 512 * k2 + 128 * k1
+                out_ref[c, :, first : first + 128] = pair[c][16 * k1 : 16 * k1 + 16]
+
+
+def image_kernel(*refs):
+    inputs, out_ref, refs = refs[:15], refs[15], refs[16:]
+    local, refs = refs[:15], refs[15:]
+    own_vis, own_tiles, own_offs, kern = local[:4]
+    (
+        got_vis, got_tiles, got_offs, tab, bt, at, sa, sb, acc, accs, spill_out, spill_in, blocks, received,
+        load_sems, send_sems, recv_sems, spill_sems, block_sems,
+    ) = refs
     slab, g = lax.axis_index("rows"), lax.axis_index("grp")
-    slabs = lax.axis_size("rows")
+    slabs, groups = lax.axis_size("rows"), lax.axis_size("grp")
+    n_dev = slabs * groups
     after, before = lax.rem(slab + 1, slabs), lax.rem(slab + slabs - 1, slabs)
     low = lax.rem(g, 2)
     sibling = g + 1 - 2 * low
     across = lax.rem(g + 2, 4)
+    me = slab * groups + g
+
+    def peer(t):
+        z = lax.rem(slab // 8 + lax.rem(t, 8), 8)
+        x = lax.rem((slab // 2) % 4 + lax.rem(t // 8, 4), 4)
+        y = lax.rem((g // 2) * 2 + slab % 2 + lax.rem(t // 32, 4), 4)
+        core = lax.rem(low + t // 128, 2)
+        return z * 8 + x * 2 + y % 2, (y // 2) * 2 + core
+
+    loads = []
+    for n, (source, target) in enumerate(zip(inputs, local)):
+        loads.append(pltpu.make_async_copy(source, target, load_sems.at[n]))
+        loads[-1].start()
 
     barrier = pltpu.get_barrier_semaphore()
-    for peer in ((slab, sibling), (slab, across), (after, g), (before, g)):
-        pl.semaphore_signal(barrier, inc=1, device_id=peer, device_id_type=MESH)
-
-    build_tables(kern, g, tab)
+
+    def greet(t, _):
+        pl.semaphore_signal(barrier, inc=1, device_id=peer(t), device_id_type=MESH)
+        return 0
+
+    lax.fori_loop(1, n_dev, greet, 0)
+
     acc[...] = jnp.zeros_like(acc)
     accs[...] = jnp.zeros_like(accs)
-    pl.semaphore_wait(barrier, 4)
-
-    def send(sources, slot, peer):
+    for load in loads[:4]:
+        load.wait()
+    build_tables(kern, g, tab)
+
+    def send(sources, slot, to):
         copies = []
         for n, (source, target) in enumerate(zip(sources, (got_vis, got_tiles, got_offs))):
             copies.append(
@@ -226,7 +294,7 @@
                     dst_ref=target.at[slot],
                     send_sem=send_sems.at[slot, n],
                     recv_sem=recv_sems.at[slot, n],
-                    device_id=(slab, peer),
+                    device_id=(slab, to),
                     device_id_type=MESH,
                 )
             )
@@ -234,16 +302,17 @@
             copy.start()
         return copies
 
-    own = (vis, tiles, offs)
+    own = (own_vis, own_tiles, own_offs)
     held = [own] + [(got_vis.at[n], got_tiles.at[n], got_offs.at[n]) for n in range(3)]
+    scratch = (bt, at, sa, sb, acc, accs)
+
+    def block(n, main, spill):
+        grid_block(*held[n], slab, g, tab, scratch, main, spill)
+
+    block(0, True, True)
+    pl.semaphore_wait(barrier, n_dev - 1)
     to_across = send(own, 1, across)
     to_sibling = send(own, 0, sibling)
-    scratch = (bt, at, sa, sb, acc, accs)
-
-    def block(n, main, spill):
-        grid_block(*held[n], slab, g, tab, scratch, main, spill)
-
-    block(0, True, True)
     for copy in to_sibling:
         copy.wait_recv()
     block(1, True, True)
@@ -268,9 +337,33 @@
     block(3, True, False)
     spill_copy.wait_recv()
     add_spill(acc, spill_in)
-    row_transform(acc, d_hi, d_lo, tw, w_hi, w_lo, out_ref)
+    for load in loads[4:]:
+        load.wait()
+    row_transform(acc, *local[4:9], blocks)
+
+    def block_copy(source, target, to):
+        return pltpu.make_async_remote_copy(
+            src_ref=blocks.at[source],
+            dst_ref=received.at[target],
+            send_sem=block_sems.at[0],
+            recv_sem=block_sems.at[1],
+            device_id=to,
+            device_id_type=MESH,
+        )
+
+    def send_block(t, _):
+        row, col = peer(t)
+        block_copy(row * groups + col, me, (row, col)).start()
+        return 0
+
+    lax.fori_loop(1, n_dev, send_block, 0)
+    received[me] = blocks[me]
+    everything = block_copy(pl.ds(0, n_dev - 1), pl.ds(0, n_dev - 1), (slab, sibling))
+    everything.wait_recv()
+    column_transform(received, *local[9:], out_ref)
     for copy in to_sibling + to_across + relayed + [spill_copy]:
         copy.wait_send()
+    everything.wait_send()
 
 
 def vmem(shape, dtype):
@@ -291,94 +384,41 @@
     ]
 
 
-def row_stage(visibilities, uv_tiles, kernel_offsets, kernel):
-    in_vmem = pl.BlockSpec(memory_space=pltpu.VMEM)
+def shards(visibilities, uv_tiles, kernel_offsets, kernel):
+    in_hbm = pl.BlockSpec(memory_space=pltpu.HBM)
+    tables = tables_v() + tables_u()
     return pl.pallas_call(
-        grid_kernel,
-        out_shape=jax.ShapeDtypeStruct((1024, 128), F32),
-        in_specs=[in_vmem] * 3 + [pl.BlockSpec(memory_space=pltpu.SMEM)] + [in_vmem] * 5,
-        out_specs=in_vmem,
+        image_kernel,
+        out_shape=jax.ShapeDtypeStruct((2, 16, G), F32),
+        in_specs=[in_hbm] * 15,
+        out_specs=pl.BlockSpec(memory_space=pltpu.VMEM),
         scratch_shapes=[
+            vmem((2, N_VIS), F32),
+            vmem((2, N_VIS), jnp.int32),
+            vmem((2, N_VIS), jnp.int32),
+            pltpu.SMEM((8, 8), F32),
+        ]
+        + [vmem(t.shape, t.dtype) for t in tables]
+        + [
             vmem((3, 2, N_VIS), F32),
             vmem((3, 2, N_VIS), jnp.int32),
             vmem((3, 2, N_VIS), jnp.int32),
         ]
         + grid_scratch()
         + [
+            vmem((256, 4, 128), F32),
+            vmem((256, 4, 128), F32),
+            pltpu.SemaphoreType.DMA((15,)),
             pltpu.SemaphoreType.DMA((3, 3)),
             pltpu.SemaphoreType.DMA((3, 3)),
             pltpu.SemaphoreType.DMA((2,)),
+            pltpu.SemaphoreType.DMA((2,)),
         ],
         compiler_params=pltpu.CompilerParams(
-            collective_id=0, has_side_effects=True, vmem_limit_bytes=50 * 2**20
+            collective_id=0, has_side_effects=True, vmem_limit_bytes=67_043_328
         ),
-        name="grid_rows",
-    )(visibilities, uv_tiles, kernel_offsets, kernel, *tables_v())
-
-
-def fft8(x):
-    def add(a, b):
-        return (a[0] + b[0], a[1] + b[1])
-
-    def sub(a, b):
-        return (a[0] - b[0], a[1] - b[1])
-
-    def by_i(a):
-        return (-a[1], a[0])
-
-    def fft4(a):
-        s, d = add(a[0], a[2]), sub(a[0], a[2])
-        t, e = add(a[1], a[3]), by_i(sub(a[1], a[3]))
-        return [add(s, t), add(d, e), sub(s, t), sub(d, e)]
-
-    root = np.float32(np.sqrt(0.5))
-    even, odd = fft4(x[0::2]), fft4(x[1::2])
-    one, three = odd[1], odd[3]
-    odd[1] = (root * (one[0] - one[1]), root * (one[0] + one[1]))
-    odd[2] = by_i(odd[2])
-    odd[3] = (root * (-three[0] - three[1]), root * (three[0] - three[1]))
-    return [add(even[k], odd[k]) for k in range(4)] + [sub(even[k], odd[k]) for k in range(4)]
-
-
-def column_kernel(r_ref, e_hi, e_lo, tw1, d_hi, d_lo, tw2, out_ref):
-    sums = []
-    for j in range(8):
-        b, g = divmod(j, 4)
-        x = jnp.concatenate([r_ref[pl.ds(4 * g + 2 * c + b, 64, stride=16), :] for c in range(2)], axis=0)
-        z = dot3((e_hi[...], e_lo[...]), halves(x), NN)
-        real, imag = z[:128], z[128:]
-        cos, sin = tw1[0], tw1[1]
-        turned = jnp.concatenate([real * cos - imag * sin, real * sin + imag * cos], axis=0)
-        p = dot3((d_hi[...], d_lo[...]), halves(turned), NT)
-        real = p[:64, :128] - p[64:, 128:]
-        imag = p[:64, 128:] + p[64:, :128]
-        cos = jnp.concatenate([jnp.broadcast_to(tw2[0, 4 * j + k : 4 * j + k + 1], (16, 128)) for k in range(4)], axis=0)
-        sin = jnp.concatenate([jnp.broadcast_to(tw2[1, 4 * j + k : 4 * j + k + 1], (16, 128)) for k in range(4)], axis=0)
-        sums.append((real * cos - imag * sin, real * sin + imag * cos))
-    for k2, pair in enumerate(fft8(sums)):
-        for c in range(2):
-            for k1 in range(4):
-                first = 512 * k2 + 128 * k1
-                out_ref[c, :, first : first + 128] = pair[c][16 * k1 : 16 * k1 + 16]
-
-
-def column_stage(received):
-    return pl.pallas_call(
-        column_kernel,
-        out_shape=jax.ShapeDtypeStruct((2, 16, G), F32),
-        in_specs=[pl.BlockSpec(memory_space=pltpu.VMEM)] * 7,
-        out_specs=pl.BlockSpec(memory_space=pltpu.VMEM),
-        compiler_params=pltpu.CompilerParams(vmem_limit_bytes=40 * 2**20),
-        name="columns",
-    )(received, *tables_u())
-
-
-def shards(visibilities, uv_tiles, kernel_offsets, kernel):
-    blocks = row_stage(visibilities, uv_tiles, kernel_offsets, kernel)
-    received = lax.all_to_all(
-        blocks.reshape(256, 4, 128), ("rows", "grp"), split_axis=0, concat_axis=0, tiled=True
-    )
-    return column_stage(received.reshape(1024, 128))
+        name="dirty_image",
+    )(visibilities, uv_tiles, kernel_offsets, kernel, *tables)
 
 
 def solution(mesh):

time: 69.4 us -> 61.3 us (0.88)
  blocking collectives: 27.1 us -> 0 us
  Pallas kernels: 33.7 us -> 59.2 us
  local copies, waits for them, and re-layouts: 7.94 us -> 1.87 us
    all_to_all x1 -> x0, blocking collectives: 27.1 us -> none  [shards(): lax.all_to_all(blocks.reshape(256, 4, 128), ('rows', 'grp'), split_axis=0...]
    pallas_call x2 -> x1, Pallas kernels: 33.7 us -> 59.2 us  [shards(): pl.pallas_call(image_kernel, out_shape=jax.ShapeDtypeStruct((2, 16, G), F...]
    unnamed x30 -> x1, local copies, waits for them, and re-layouts: 7.94 us -> 1.87 us
where the time goes in v2:
time: 61.3 us; the launch traced here: 61.1 us
  Pallas kernels  59.2 us (97%)
  local copies, waits for them, and re-layouts  1.87 us (3%)
    pallas_call x1, Pallas kernels, shards(): pl.pallas_call(image_kernel, out_shape=jax.ShapeDtypeStruct((2, 16, G), F...  59.2 us
    unnamed x1, local copies, waits for them, and re-layouts  1.87 us

profile of v2, /device:TPU:1, one launch (start us, length us, event | category | flops | bytes accessed | tf_op | source)
XLA Modules:
  0.0 61.1 jit_solution(8357707181329574307)
XLA Ops:
  0.0 59.2 %dirty_image.1 = f32[2,16,4096]{2,1,0:T(8,128)} custom-call(f32[2,4096]{1,0:T(2,128)} %refs_0_.1, s32[2,4096]{1,0:T(2,128)} %refs_1_.1, s32[2,4096]{1,0:T(2,128)} %refs_2_.1, f32[8,8]{1,0:T(8,128)} %refs_3_.1, bf16[256,512]{1,0:T(8,128)(2,1)} %constant.22.clone.refs_4_, bf16[256,512]{1,0:T(8,128)(2,1)} %constant.23.clone.refs_5_, ...), custom_call_target="tpu_custom_call" | custom-call | tf_op jit(solution)/shard_map/dirty_image/pallas_call | solution.py:390
  59.2 1.9 %copy.17 = f32[2,16,4096]{2,1,0:T(8,128)} copy(f32[2,16,4096]{2,1,0:T(8,128)} %dirty_image.1) | data formatting | bytes 1048576

commit v3 on v2

--- a/solution.py
+++ b/solution.py
@@ -9,7 +9,7 @@
 from jax.sharding import PartitionSpec as P
 
 G = 4096
-MESH = pl.DeviceIdType.MESH
+LOGICAL = pl.DeviceIdType.LOGICAL
 BF16 = jnp.bfloat16
 F32 = jnp.float32
 CHUNK = 1024
@@ -248,23 +248,15 @@
     own_vis, own_tiles, own_offs, kern = local[:4]
     (
         got_vis, got_tiles, got_offs, tab, bt, at, sa, sb, acc, accs, spill_out, spill_in, blocks, received,
-        load_sems, send_sems, recv_sems, spill_sems, block_sems,
+        load_sems, send_sems, recv_sems, spill_sems, block_sems, plane_sem, all_sem,
     ) = refs
     slab, g = lax.axis_index("rows"), lax.axis_index("grp")
     slabs, groups = lax.axis_size("rows"), lax.axis_size("grp")
     n_dev = slabs * groups
     after, before = lax.rem(slab + 1, slabs), lax.rem(slab + slabs - 1, slabs)
-    low = lax.rem(g, 2)
-    sibling = g + 1 - 2 * low
-    across = lax.rem(g + 2, 4)
     me = slab * groups + g
-
-    def peer(t):
-        z = lax.rem(slab // 8 + lax.rem(t, 8), 8)
-        x = lax.rem((slab // 2) % 4 + lax.rem(t // 8, 4), 4)
-        y = lax.rem((g // 2) * 2 + slab % 2 + lax.rem(t // 32, 4), 4)
-        core = lax.rem(low + t // 128, 2)
-        return z * 8 + x * 2 + y % 2, (y // 2) * 2 + core
+    sibling, across = me ^ 1, me ^ 2
+    after, before = after * groups + g, before * groups + g
 
     loads = []
     for n, (source, target) in enumerate(zip(inputs, local)):
@@ -273,11 +265,11 @@
 
     barrier = pltpu.get_barrier_semaphore()
 
-    def greet(t, _):
-        pl.semaphore_signal(barrier, inc=1, device_id=peer(t), device_id_type=MESH)
-        return 0
-
-    lax.fori_loop(1, n_dev, greet, 0)
+    line_x = [me ^ (8 * x) for x in range(1, 4)]
+    line_z = [me ^ (32 * z) for z in range(1, 8)]
+    first = [me ^ y for y in range(1, 8)] + line_x + line_z + [after, before]
+    for to in first:
+        pl.semaphore_signal(barrier, inc=1, device_id=to, device_id_type=LOGICAL)
 
     acc[...] = jnp.zeros_like(acc)
     accs[...] = jnp.zeros_like(accs)
@@ -294,8 +286,8 @@
                     dst_ref=target.at[slot],
                     send_sem=send_sems.at[slot, n],
                     recv_sem=recv_sems.at[slot, n],
-                    device_id=(slab, to),
-                    device_id_type=MESH,
+                    device_id=to,
+                    device_id_type=LOGICAL,
                 )
             )
         for copy in copies:
@@ -309,10 +301,15 @@
     def block(n, main, spill):
         grid_block(*held[n], slab, g, tab, scratch, main, spill)
 
-    block(0, True, True)
-    pl.semaphore_wait(barrier, n_dev - 1)
+    pl.semaphore_wait(barrier, len(first))
     to_across = send(own, 1, across)
     to_sibling = send(own, 0, sibling)
+    for to in line_x:
+        pl.semaphore_signal(plane_sem, inc=1, device_id=to, device_id_type=LOGICAL)
+    block(0, True, True)
+    pl.semaphore_wait(plane_sem, len(line_x))
+    for to in line_z:
+        pl.semaphore_signal(all_sem, inc=1, device_id=to, device_id_type=LOGICAL)
     for copy in to_sibling:
         copy.wait_recv()
     block(1, True, True)
@@ -329,8 +326,8 @@
         dst_ref=spill_in,
         send_sem=spill_sems.at[0],
         recv_sem=spill_sems.at[1],
-        device_id=(after, g),
-        device_id_type=MESH,
+        device_id=after,
+        device_id_type=LOGICAL,
     )
     spill_copy.start()
     block(2, True, False)
@@ -339,6 +336,7 @@
     add_spill(acc, spill_in)
     for load in loads[4:]:
         load.wait()
+    pl.semaphore_wait(all_sem, len(line_z))
     row_transform(acc, *local[4:9], blocks)
 
     def block_copy(source, target, to):
@@ -348,17 +346,23 @@
             send_sem=block_sems.at[0],
             recv_sem=block_sems.at[1],
             device_id=to,
-            device_id_type=MESH,
+            device_id_type=LOGICAL,
         )
 
-    def send_block(t, _):
-        row, col = peer(t)
-        block_copy(row * groups + col, me, (row, col)).start()
+    def send_block(t):
+        to = me ^ t
+        block_copy(to, me, to).start()
+
+    def send_blocks(low, _):
+        for z in range(8):
+            send_block(low ^ (32 * z))
         return 0
 
-    lax.fori_loop(1, n_dev, send_block, 0)
+    for z in range(1, 8):
+        send_block(32 * z)
+    lax.fori_loop(1, n_dev // 8, send_blocks, 0)
     received[me] = blocks[me]
-    everything = block_copy(pl.ds(0, n_dev - 1), pl.ds(0, n_dev - 1), (slab, sibling))
+    everything = block_copy(pl.ds(0, n_dev - 1), pl.ds(0, n_dev - 1), sibling)
     everything.wait_recv()
     column_transform(received, *local[9:], out_ref)
     for copy in to_sibling + to_across + relayed + [spill_copy]:
@@ -413,6 +417,8 @@
             pltpu.SemaphoreType.DMA((3, 3)),
             pltpu.SemaphoreType.DMA((2,)),
             pltpu.SemaphoreType.DMA((2,)),
+            pltpu.SemaphoreType.REGULAR,
+            pltpu.SemaphoreType.REGULAR,
         ],
         compiler_params=pltpu.CompilerParams(
             collective_id=0, has_side_effects=True, vmem_limit_bytes=67_043_328

time: 61.3 us -> 48.2 us (0.79)
  Pallas kernels: 59.2 us -> 46.1 us
    pallas_call x1, Pallas kernels: 59.2 us -> 46.1 us  [shards(): pl.pallas_call(image_kernel, out_shape=jax.ShapeDtypeStruct((2, 16, G), F...]
where the time goes in v3:
time: 48.2 us; the launch traced here: 48 us
  Pallas kernels  46.1 us (96%)
  local copies, waits for them, and re-layouts  1.87 us (4%)
    pallas_call x1, Pallas kernels, shards(): pl.pallas_call(image_kernel, out_shape=jax.ShapeDtypeStruct((2, 16, G), F...  46.1 us
    unnamed x1, local copies, waits for them, and re-layouts  1.87 us

profile of v3, /device:TPU:1, one launch (start us, length us, event | category | flops | bytes accessed | tf_op | source)
XLA Modules:
  0.0 48.0 jit_solution(11372844644028204140)
XLA Ops:
  0.0 46.1 %dirty_image.1 = f32[2,16,4096]{2,1,0:T(8,128)} custom-call(f32[2,4096]{1,0:T(2,128)} %refs_0_.1, s32[2,4096]{1,0:T(2,128)} %refs_1_.1, s32[2,4096]{1,0:T(2,128)} %refs_2_.1, f32[8,8]{1,0:T(8,128)} %refs_3_.1, bf16[256,512]{1,0:T(8,128)(2,1)} %constant.22.clone.refs_4_, bf16[256,512]{1,0:T(8,128)(2,1)} %constant.23.clone.refs_5_, ...), custom_call_target="tpu_custom_call" | custom-call | tf_op jit(solution)/shard_map/dirty_image/pallas_call | solution.py:394
  46.1 1.9 %copy.17 = f32[2,16,4096]{2,1,0:T(8,128)} copy(f32[2,16,4096]{2,1,0:T(8,128)} %dirty_image.1) | data formatting | bytes 1048576

commit v4 on v3

--- a/solution.py
+++ b/solution.py
@@ -12,10 +12,10 @@
 LOGICAL = pl.DeviceIdType.LOGICAL
 BF16 = jnp.bfloat16
 F32 = jnp.float32
-CHUNK = 1024
+CHUNK = 2048
 N_VIS = 4096
 ROWS_W = 272
-ROWS_S = 48
+ROWS_S = 80
 
 
 def split_table(x):
@@ -119,23 +119,19 @@
         if bt is not None or sb is not None:
             taps = pick(wide(off_col, 8), tab_ref, 0)
             wrapped = (sub8 < off_col).astype(jnp.int32)
-            carry = jnp.concatenate([wrapped, wrapped], axis=0) - half
-            values = []
-            for c in range(2):
-                one = vis_ref[c : c + 1, here] * taps
-                values.append(jnp.concatenate([one, one], axis=0).astype(BF16))
+            one_of = [vis_ref[c : c + 1, here] * taps for c in range(2)]
         if bt is not None:
-            need = as_bf16(carry + (tile_col & 31))
+            need = as_bf16(jnp.concatenate([wrapped, wrapped], axis=0) - half + (tile_col & 31))
+            values = [jnp.concatenate([one, one], axis=0).astype(BF16) for one in one_of]
             for m in range(17):
                 hit = need == BF16(2 * m)
                 for c in range(2):
                     bt[c * ROWS_W + 16 * m : c * ROWS_W + 16 * m + 16, lanes] = jnp.where(hit, values[c], zero)
         if sb is not None:
-            need = as_bf16(carry + (tile_col & 3))
-            for m in range(3):
-                hit = need == BF16(2 * m)
-                for c in range(2):
-                    sb[c * ROWS_S + 16 * m : c * ROWS_S + 16 * m + 16, lanes] = jnp.where(hit, values[c], zero)
+            need = as_bf16(jnp.concatenate([wrapped, wrapped], axis=0) + (tile_col & 3))
+            pair = jnp.concatenate([one_of[0], one_of[1]], axis=0).astype(BF16)
+            for m in range(5):
+                sb[16 * m : 16 * m + 16, lanes] = jnp.where(need == BF16(m), pair, zero)
         if at is not None or sa is not None:
             row_taps = pick(wide(off_row, 8), tab_ref, 8)
             own_h = sub16 == wide(tile_col >> 5, 16)
@@ -155,30 +151,33 @@
                         sa[first : first + 16, lanes] = jnp.where(need == BF16(t), spread, zero)
 
 
-def grid_block(vis_ref, tile_ref, off_ref, slab, g, tab_ref, scratch, main, spill):
+def grid_blocks(slots, vis, tiles, offs, slab, g, tab_ref, scratch, main, spill):
     bt, at, sa, sb, acc, accs = scratch
+    parts = ((bt, at) if main else (None, None)) + ((sa, sb) if spill else (None, None))
+    per_slot = N_VIS // CHUNK
 
     def step(i, _):
-        start = pl.multiple_of(i * CHUNK, CHUNK)
-        parts = (bt if main else None, at if main else None, sa if spill else None, sb if spill else None)
-        build(vis_ref, tile_ref, off_ref, start, slab, g, tab_ref, parts)
+        slot = i // per_slot
+        start = pl.multiple_of(lax.rem(i, per_slot) * CHUNK, CHUNK)
+        build(vis.at[slot], tiles.at[slot], offs.at[slot], start, slab, g, tab_ref, parts)
         if main:
             acc[...] += dot(bt[...], at[...], NT)
         if spill:
             accs[...] += dot(sa[...], sb[...], NT)
         return 0
 
-    lax.fori_loop(0, N_VIS // CHUNK, step, 0)
+    lax.fori_loop(slots[0] * per_slot, slots[1] * per_slot, step, 0)
 
 
 def add_spill(acc, got):
     for c in range(2):
         for b in range(2):
             for f in range(8):
-                rows = pl.ds(c * ROWS_W + 32 * f, ROWS_S)
-                acc[rows, b * 128 : b * 128 + 16] += got[
-                    c * ROWS_S : (c + 1) * ROWS_S, b * 128 + f * 16 : b * 128 + f * 16 + 16
-                ]
+                first = c * ROWS_W + 32 * f
+                for m in range(5):
+                    acc[first + 8 * m : first + 8 * m + 8, b * 128 : b * 128 + 16] += got[
+                        16 * m + 8 * c : 16 * m + 8 * c + 8, b * 128 + f * 16 : b * 128 + f * 16 + 16
+                    ]
 
 
 def row_transform(acc, d_hi, d_lo, tw, w_hi, w_lo, out_ref):
@@ -242,12 +241,12 @@
                 out_ref[c, :, first : first + 128] = pair[c][16 * k1 : 16 * k1 + 16]
 
 
-def image_kernel(*refs):
-    inputs, out_ref, refs = refs[:15], refs[15], refs[16:]
-    local, refs = refs[:15], refs[15:]
-    own_vis, own_tiles, own_offs, kern = local[:4]
+def row_kernel(*refs):
+    inputs, received, refs = refs[:9], refs[9], refs[10:]
+    held, local, refs = refs[:3], refs[3:9], refs[9:]
+    kern, tables = local[0], local[1:]
     (
-        got_vis, got_tiles, got_offs, tab, bt, at, sa, sb, acc, accs, spill_out, spill_in, blocks, received,
+        tab, bt, at, sa, sb, acc, accs, spill_out, spill_in, blocks,
         load_sems, send_sems, recv_sems, spill_sems, block_sems, plane_sem, all_sem,
     ) = refs
     slab, g = lax.axis_index("rows"), lax.axis_index("grp")
@@ -259,7 +258,7 @@
     after, before = after * groups + g, before * groups + g
 
     loads = []
-    for n, (source, target) in enumerate(zip(inputs, local)):
+    for n, (source, target) in enumerate(zip(inputs, [h.at[0] for h in held] + list(local))):
         loads.append(pltpu.make_async_copy(source, target, load_sems.at[n]))
         loads[-1].start()
 
@@ -277,15 +276,15 @@
         load.wait()
     build_tables(kern, g, tab)
 
-    def send(sources, slot, to):
+    def send(source, target, to):
         copies = []
-        for n, (source, target) in enumerate(zip(sources, (got_vis, got_tiles, got_offs))):
+        for n, ref in enumerate(held):
             copies.append(
                 pltpu.make_async_remote_copy(
-                    src_ref=source,
-                    dst_ref=target.at[slot],
-                    send_sem=send_sems.at[slot, n],
-                    recv_sem=recv_sems.at[slot, n],
+                    src_ref=ref.at[source],
+                    dst_ref=ref.at[target],
+                    send_sem=send_sems.at[target - 1, n],
+                    recv_sem=recv_sems.at[target - 1, n],
                     device_id=to,
                     device_id_type=LOGICAL,
                 )
@@ -294,32 +293,27 @@
             copy.start()
         return copies
 
-    own = (own_vis, own_tiles, own_offs)
-    held = [own] + [(got_vis.at[n], got_tiles.at[n], got_offs.at[n]) for n in range(3)]
     scratch = (bt, at, sa, sb, acc, accs)
 
-    def block(n, main, spill):
-        grid_block(*held[n], slab, g, tab, scratch, main, spill)
+    def grid(first_slot, end_slot, main, spill):
+        grid_blocks((first_slot, end_slot), *held, slab, g, tab, scratch, main, spill)
 
     pl.semaphore_wait(barrier, len(first))
-    to_across = send(own, 1, across)
-    to_sibling = send(own, 0, sibling)
+    to_across = send(0, 2, across)
+    to_sibling = send(0, 1, sibling)
     for to in line_x:
         pl.semaphore_signal(plane_sem, inc=1, device_id=to, device_id_type=LOGICAL)
-    block(0, True, True)
+    grid(0, 1, True, True)
     pl.semaphore_wait(plane_sem, len(line_x))
     for to in line_z:
         pl.semaphore_signal(all_sem, inc=1, device_id=to, device_id_type=LOGICAL)
-    for copy in to_sibling:
+    for copy in to_sibling + to_across:
         copy.wait_recv()
-    block(1, True, True)
-    for copy in to_across:
-        copy.wait_recv()
-    relayed = send(held[2], 2, sibling)
-    block(2, False, True)
+    relayed = send(2, 3, sibling)
+    grid(1, 3, True, True)
     for copy in relayed:
         copy.wait_recv()
-    block(3, False, True)
+    grid(3, 4, False, True)
     spill_out[...] = accs[...].T
     spill_copy = pltpu.make_async_remote_copy(
         src_ref=spill_out,
@@ -330,14 +324,13 @@
         device_id_type=LOGICAL,
     )
     spill_copy.start()
-    block(2, True, False)
-    block(3, True, False)
+    grid(3, 4, True, False)
     spill_copy.wait_recv()
     add_spill(acc, spill_in)
     for load in loads[4:]:
         load.wait()
     pl.semaphore_wait(all_sem, len(line_z))
-    row_transform(acc, *local[4:9], blocks)
+    row_transform(acc, *tables, blocks)
 
     def block_copy(source, target, to):
         return pltpu.make_async_remote_copy(
@@ -353,6 +346,9 @@
         to = me ^ t
         block_copy(to, me, to).start()
 
+    own_copy = pltpu.make_async_copy(blocks.at[me], received.at[me], load_sems.at[0])
+    own_copy.start()
+
     def send_blocks(low, _):
         for z in range(8):
             send_block(low ^ (32 * z))
@@ -361,10 +357,9 @@
     for z in range(1, 8):
         send_block(32 * z)
     lax.fori_loop(1, n_dev // 8, send_blocks, 0)
-    received[me] = blocks[me]
+    own_copy.wait()
     everything = block_copy(pl.ds(0, n_dev - 1), pl.ds(0, n_dev - 1), sibling)
     everything.wait_recv()
-    column_transform(received, *local[9:], out_ref)
     for copy in to_sibling + to_across + relayed + [spill_copy]:
         copy.wait_send()
     everything.wait_send()
@@ -380,39 +375,43 @@
         vmem((2 * ROWS_W, CHUNK), BF16),
         vmem((256, CHUNK), BF16),
         vmem((256, CHUNK), BF16),
-        vmem((2 * ROWS_S, CHUNK), BF16),
+        vmem((ROWS_S, CHUNK), BF16),
         vmem((2 * ROWS_W, 256), F32),
-        vmem((256, 2 * ROWS_S), F32),
-        vmem((2 * ROWS_S, 256), F32),
-        vmem((2 * ROWS_S, 256), F32),
+        vmem((256, ROWS_S), F32),
+        vmem((ROWS_S, 256), F32),
+        vmem((ROWS_S, 256), F32),
     ]
+
+
+def column_kernel(*refs):
+    inputs, out_ref, local, sems = refs[:7], refs[7], refs[8:15], refs[15]
+    loads = [pltpu.make_async_copy(a, b, sems.at[n]) for n, (a, b) in enumerate(zip(inputs, local))]
+    for load in loads:
+        load.start()
+    for load in loads:
+        load.wait()
+    column_transform(*local, out_ref)
 
 
 def shards(visibilities, uv_tiles, kernel_offsets, kernel):
     in_hbm = pl.BlockSpec(memory_space=pltpu.HBM)
-    tables = tables_v() + tables_u()
-    return pl.pallas_call(
-        image_kernel,
-        out_shape=jax.ShapeDtypeStruct((2, 16, G), F32),
-        in_specs=[in_hbm] * 15,
-        out_specs=pl.BlockSpec(memory_space=pltpu.VMEM),
+    tables = tables_v()
+    received = pl.pallas_call(
+        row_kernel,
+        out_shape=jax.ShapeDtypeStruct((256, 4, 128), F32),
+        in_specs=[in_hbm] * 9,
+        out_specs=in_hbm,
         scratch_shapes=[
-            vmem((2, N_VIS), F32),
-            vmem((2, N_VIS), jnp.int32),
-            vmem((2, N_VIS), jnp.int32),
+            vmem((4, 2, N_VIS), F32),
+            vmem((4, 2, N_VIS), jnp.int32),
+            vmem((4, 2, N_VIS), jnp.int32),
             pltpu.SMEM((8, 8), F32),
         ]
         + [vmem(t.shape, t.dtype) for t in tables]
-        + [
-            vmem((3, 2, N_VIS), F32),
-            vmem((3, 2, N_VIS), jnp.int32),
-            vmem((3, 2, N_VIS), jnp.int32),
-        ]
         + grid_scratch()
         + [
             vmem((256, 4, 128), F32),
-            vmem((256, 4, 128), F32),
-            pltpu.SemaphoreType.DMA((15,)),
+            pltpu.SemaphoreType.DMA((9,)),
             pltpu.SemaphoreType.DMA((3, 3)),
             pltpu.SemaphoreType.DMA((3, 3)),
             pltpu.SemaphoreType.DMA((2,)),
@@ -423,8 +422,20 @@
         compiler_params=pltpu.CompilerParams(
             collective_id=0, has_side_effects=True, vmem_limit_bytes=67_043_328
         ),
-        name="dirty_image",
+        name="row_spectra",
     )(visibilities, uv_tiles, kernel_offsets, kernel, *tables)
+    tables = tables_u()
+    return pl.pallas_call(
+        column_kernel,
+        out_shape=jax.ShapeDtypeStruct((2, 16, G), F32),
+        in_specs=[in_hbm] * 7,
+        out_specs=pl.BlockSpec(memory_space=pltpu.VMEM),
+        scratch_shapes=[vmem((256, 4, 128), F32)]
+        + [vmem(t.shape, t.dtype) for t in tables]
+        + [pltpu.SemaphoreType.DMA((7,))],
+        compiler_params=pltpu.CompilerParams(vmem_limit_bytes=67_043_328),
+        name="column_spectra",
+    )(received, *tables)
 
 
 def solution(mesh):

time: 48.2 us -> 46.7 us (0.969)
  local copies, waits for them, and re-layouts: 1.87 us -> 0 us
  Pallas kernels: 46.1 us -> 46.6 us
    unnamed x1 -> x0, local copies, waits for them, and re-layouts: 1.87 us -> none
    pallas_call x1 -> x2, Pallas kernels: 46.1 us -> 46.6 us  [the longest x1 43.3 us: shards(): pl.pallas_call(row_kernel, out_shape=jax.ShapeDtypeStruct((256, 4, 128),...]
where the time goes in v4:
time: 46.7 us; the launch traced here: 46.6 us
  Pallas kernels  46.6 us (100%)
    pallas_call x1, Pallas kernels, shards(): pl.pallas_call(row_kernel, out_shape=jax.ShapeDtypeStruct((256, 4, 128),...  43.3 us
    pallas_call x1, Pallas kernels, shards(): pl.pallas_call(column_kernel, out_shape=jax.ShapeDtypeStruct((2, 16, G),...  3.25 us

profile of v4, /device:TPU:1, one launch (start us, length us, event | category | flops | bytes accessed | tf_op | source)
XLA Modules:
  0.0 46.6 jit_solution(15317472264143619586)
XLA Ops:
  0.0 43.3 %row_spectra.1.refs_0_ = f32[256,4,128]{2,1,0:T(4,128)} custom-call(f32[2,4096]{1,0:T(2,128)} %refs_0_.1, s32[2,4096]{1,0:T(2,128)} %refs_1_.2, s32[2,4096]{1,0:T(2,128)} %refs_2_.2, f32[8,8]{1,0:T(8,128)} %refs_3_.2, bf16[256,512]{1,0:T(8,128)(2,1)} %constant.22.clone.refs_4_, bf16[256,512]{1,0:T(8,128)(2,1)} %constant.23.clone.refs_5_, ...), custom_call_target="tpu_custom_call" | custom-call | tf_op jit(solution)/shard_map/row_spectra/pallas_call | solution.py:399
  43.4 3.3 %column_spectra.1 = f32[2,16,4096]{2,1,0:T(8,128)} custom-call(f32[256,4,128]{2,1,0:T(4,128)} %row_spectra.1.refs_0_, bf16[256,128]{1,0:T(8,128)(2,1)} %constant.27.clone.refs_1_, bf16[256,128]{1,0:T(8,128)(2,1)} %constant.28.clone.refs_2_, f32[2,128,128]{2,1,0:T(8,128)} %constant.29.clone.refs_3_, bf16[128,128]{1,0:T(8,128)(2,1)} %constant.30.clone.refs_4_, ...), custom_call_target="tpu_custom_call" | custom-call | tf_op jit(solution)/shard_map/column_spectra/pallas_call | solution.py:428

commit v5 on v4

--- a/solution.py
+++ b/solution.py
@@ -12,7 +12,7 @@
 LOGICAL = pl.DeviceIdType.LOGICAL
 BF16 = jnp.bfloat16
 F32 = jnp.float32
-CHUNK = 2048
+CHUNK = 4096
 N_VIS = 4096
 ROWS_W = 272
 ROWS_S = 80
@@ -71,6 +71,11 @@
 
 def dot3(a, b, dims):
     return dot(a[0], b[0], dims) + (dot(a[1], b[0], dims) + dot(a[0], b[1], dims))
+
+
+def dot2(table, x, dims):
+    x = x.astype(BF16)
+    return dot(table[0], x, dims) + dot(table[1], x, dims)
 
 
 NN = ((1,), (0,))
@@ -189,7 +194,7 @@
     sin = jnp.concatenate([tw[1], tw[1]], axis=1)
     turned = (real * cos - imag * sin, real * sin + imag * cos)
     both = jnp.concatenate([jnp.concatenate([t[:16] + t[256:], t[16:256]], axis=0) for t in turned], axis=0)
-    s = dot3((w_hi[...], w_lo[...]), halves(both), NN)
+    s = dot2((w_hi[...], w_lo[...]), both, NN)
     for c in range(2):
         for b in range(2):
             out_ref[:, 2 * c + b, :] = s[c * 256 : (c + 1) * 256, b * 128 : (b + 1) * 128]
@@ -220,17 +225,23 @@
 
 
 def column_transform(r_ref, e_hi, e_lo, tw1, d_hi, d_lo, tw2, out_ref):
+    def rows_of(j):
+        b, g = divmod(j, 4)
+        return jnp.concatenate([r_ref[pl.ds(g, 64, stride=4), 2 * c + b, :] for c in range(2)], axis=0)
+
+    x = jnp.concatenate([rows_of(j) for j in range(8)], axis=1)
+    z = dot2((e_hi[...], e_lo[...]), x, NN)
+    cos, sin = tw1[0], tw1[1]
+    turned = []
+    for j in range(8):
+        real, imag = z[:128, 128 * j : 128 * j + 128], z[128:, 128 * j : 128 * j + 128]
+        turned += [real * cos - imag * sin, real * sin + imag * cos]
+    p = dot2((d_hi[...], d_lo[...]), jnp.concatenate(turned, axis=0), NT)
     sums = []
     for j in range(8):
-        b, g = divmod(j, 4)
-        x = jnp.concatenate([r_ref[pl.ds(g, 64, stride=4), 2 * c + b, :] for c in range(2)], axis=0)
-        z = dot3((e_hi[...], e_lo[...]), halves(x), NN)
-        real, imag = z[:128], z[128:]
-        cos, sin = tw1[0], tw1[1]
-        turned = jnp.concatenate([real * cos - imag * sin, real * sin + imag * cos], axis=0)
-        p = dot3((d_hi[...], d_lo[...]), halves(turned), NT)
-        real = p[:64, :128] - p[64:, 128:]
-        imag = p[:64, 128:] + p[64:, :128]
+        first, second = p[:, 256 * j : 256 * j + 128], p[:, 256 * j + 128 : 256 * j + 256]
+        real = first[:64] - second[64:]
+        imag = second[:64] + first[64:]
         cos = jnp.concatenate([jnp.broadcast_to(tw2[0, 4 * j + k : 4 * j + k + 1], (16, 128)) for k in range(4)], axis=0)
         sin = jnp.concatenate([jnp.broadcast_to(tw2[1, 4 * j + k : 4 * j + k + 1], (16, 128)) for k in range(4)], axis=0)
         sums.append((real * cos - imag * sin, real * sin + imag * cos))
@@ -350,7 +361,7 @@
     own_copy.start()
 
     def send_blocks(low, _):
-        for z in range(8):
+        for z in (4, 3, 5, 2, 6, 1, 7, 0):
             send_block(low ^ (32 * z))
         return 0
 

time: 46.7 us -> 45.8 us (0.981)
  Pallas kernels: 46.6 us -> 45.7 us
    pallas_call x1, Pallas kernels: 43.3 us -> 42.6 us  [shards(): pl.pallas_call(row_kernel, out_shape=jax.ShapeDtypeStruct((256, 4, 128),...]
where the time goes in v5:
time: 45.8 us; the launch traced here: 45.7 us
  Pallas kernels  45.7 us (100%)
    pallas_call x1, Pallas kernels, shards(): pl.pallas_call(row_kernel, out_shape=jax.ShapeDtypeStruct((256, 4, 128),...  42.6 us
    pallas_call x1, Pallas kernels, shards(): pl.pallas_call(column_kernel, out_shape=jax.ShapeDtypeStruct((2, 16, G),...  3.06 us

profile of v5, /device:TPU:1, one launch (start us, length us, event | category | flops | bytes accessed | tf_op | source)
XLA Modules:
  0.0 45.7 jit_solution(3163334402096766046)
XLA Ops:
  0.0 42.6 %row_spectra.1.refs_0_ = f32[256,4,128]{2,1,0:T(4,128)} custom-call(f32[2,4096]{1,0:T(2,128)} %refs_0_.1, s32[2,4096]{1,0:T(2,128)} %refs_1_.2, s32[2,4096]{1,0:T(2,128)} %refs_2_.2, f32[8,8]{1,0:T(8,128)} %refs_3_.2, bf16[256,512]{1,0:T(8,128)(2,1)} %constant.22.clone.refs_4_, bf16[256,512]{1,0:T(8,128)(2,1)} %constant.23.clone.refs_5_, ...), custom_call_target="tpu_custom_call" | custom-call | tf_op jit(solution)/shard_map/row_spectra/pallas_call | solution.py:410
  42.7 3.1 %column_spectra.1 = f32[2,16,4096]{2,1,0:T(8,128)} custom-call(f32[256,4,128]{2,1,0:T(4,128)} %row_spectra.1.refs_0_, bf16[256,128]{1,0:T(8,128)(2,1)} %constant.27.clone.refs_1_, bf16[256,128]{1,0:T(8,128)(2,1)} %constant.28.clone.refs_2_, f32[2,128,128]{2,1,0:T(8,128)} %constant.29.clone.refs_3_, bf16[128,128]{1,0:T(8,128)(2,1)} %constant.30.clone.refs_4_, ...), custom_call_target="tpu_custom_call" | custom-call | tf_op jit(solution)/shard_map/column_spectra/pallas_call | solution.py:439
